TPU v7x, 128 devices: a whole 4x4x4 slice. The times are simulated.
128 devices in a mesh: cls: 4 (over y), dom: 32 (over z, x, core).
Axes of the slice: x: 4, y: 4, z: 4, core: 2. Of those that a mesh axis runs over, the one named last changes fastest.
Arguments:
- particles: bfloat16 [1024, 2, 110592], P(('cls', 'dom')), may hold values from -18 to 18
- labels: int32 [1024, 1], P(('cls', 'dom')), may hold values from 0 to 7; in each aligned block of 8 rows (0 to 7, 8 to 15, ...) at most 2 rows name the same one
- wedge_index: int32 [1024], P(('cls', 'dom')), may hold values from 0 to 11
- wedge_table: float32 [12, 110592], replicated, may hold values from 0.05 to 1
Outputs:
- class_average: float32 [8, 2, 110592], P('cls', None, 'dom')
- weight_total: float32 [8, 110592], P('cls', 'dom')
Inputs may be any that keep to these rules, and one draw needn't show every extreme that they name: `labels`: among the rows of one device no class appears more than 2 times, and on some devices one class appears exactly 2 times; every class appears on some device.
All inputs are finite; a program needn't handle non-finite values.
Results may differ from a plain program's by a relative error of at most 0.0003.
Values may be sent and summed in bfloat16 or wider, within the bound.
A program may use at most 128 MiB of HBM per device.

v0:
```python
import math

import jax
import jax.numpy as jnp
from jax import lax
from jax.sharding import PartitionSpec as P

CLS_GROUP = 2


def in_order(tiles, dim):
    dims = list(tiles.shape[1:])
    dims[dim] *= tiles.shape[0]
    return jnp.moveaxis(tiles, 0, dim).reshape(dims)


def gather_packed(arrays, axis, dims):
    flat = jnp.concatenate([a.reshape(-1) for a in arrays])
    lines, at, done = (lax.all_gather(flat, axis), 0, [])
    for a, dim in zip(arrays, dims):
        tiles = lines[:, at : at + a.size].reshape(-1, *a.shape)
        done.append(in_order(tiles, dim))
        at += a.size
    return tuple(done)


def split_up(shard, dim, devices):
    before, after = (shard.shape[:dim], shard.shape[dim + 1 :])
    return jnp.moveaxis(shard.reshape(*before, devices, -1, *after), dim, 0)


def summed_on_arrival(shard, axis, dim):
    tiles = split_up(shard, dim, lax.axis_size(axis))
    arrived = lax.all_to_all(tiles, axis, split_axis=0, concat_axis=0, tiled=True)
    return arrived.sum(axis=0)


def in_one_piece(arrays, axis, dim, along):
    widths = [math.prod(a.shape[along:]) for a in arrays]
    both = jnp.concatenate(
        [a.reshape(*a.shape[:along], w) for a, w in zip(arrays, widths)], axis=along
    )
    filled = summed_on_arrival(both, axis, dim)
    tiles = jnp.split(filled, [sum(widths[:k]) for k in range(1, len(widths))], axis=along)
    return tuple(
        (b.reshape(*filled.shape[:along], *a.shape[along:]) for a, b in zip(arrays, tiles))
    )


def per_device(particles, labels, wedge_index, wedge_table):
    n_cls = lax.axis_size("cls")
    n_dom = lax.axis_size("dom")
    p_dev = particles.shape[0]
    voxels = particles.shape[2]
    shard_len = voxels // n_dom
    wedge_count = wedge_table.shape[0]
    label_flat = labels[:, 0]
    parts_four = particles.reshape(p_dev, 2, n_dom, shard_len)
    dom_pos = lax.axis_index("dom")
    table_shard = lax.dynamic_slice_in_dim(wedge_table, dom_pos * shard_len, shard_len, 1)
    got_data = lax.all_to_all(parts_four, "dom", split_axis=2, concat_axis=0, tiled=True)
    got_data = got_data.reshape(n_dom * p_dev, 2, shard_len)
    group_labels, group_wedges = gather_packed((label_flat, wedge_index), "dom", (0, 0))
    pick = (group_wedges[:, None] == jnp.arange(wedge_count, dtype=jnp.int32)[None, :]).astype(
        jnp.float32
    )
    weight = jnp.dot(pick, table_shard, precision=lax.Precision.HIGHEST)
    member = (
        jnp.arange(n_cls * CLS_GROUP, dtype=jnp.int32)[:, None] == group_labels[None, :]
    ).astype(jnp.float32)
    weighted = weight[:, None, :] * got_data
    local_sums = jnp.einsum("kp,pcv->kcv", member, weighted, precision=lax.Precision.HIGHEST)
    local_totals = jnp.dot(member, weight * weight, precision=lax.Precision.HIGHEST)
    local_sums = local_sums.reshape(n_cls, CLS_GROUP, 2, shard_len)
    local_totals = local_totals.reshape(n_cls, CLS_GROUP, shard_len)
    summed, totals = in_one_piece((local_sums, local_totals), "cls", 0, 2)
    weighted_sum = summed[0]
    weight_total = totals[0]
    class_average = weighted_sum / (weight_total[:, None, :] + 1.0)
    return (class_average, weight_total)


def solution(mesh):
    return jax.shard_map(
        per_device,
        mesh=mesh,
        in_specs=(P(("cls", "dom"), None, None), P(("cls", "dom"), None), P(("cls", "dom")), P()),
        out_specs=(P("cls", None, "dom"), P("cls", "dom")),
        check_vma=False,
    )
```

profile of v0, /device:TPU:0, one launch (start us, length us, event | category | flops | bytes accessed | tf_op | source)
XLA Modules:
  0.0 113.2 jit_solution(14025087326459504090)
XLA Ops:
  0.6 5.6 %reshape.61 = bf16[8,2,32,3456]{3,2,1,0:T(8,128)(2,1)S(1)} reshape(bf16[8,2,110592]{2,1,0:T(2,128)(2,1)} %param.4) | data formatting | bytes 7077888 | tf_op jit(solution)/shard_map/reshape | solution.py:58
  6.2 3.7 %copy.13 = bf16[8,2,32,3456]{3,0,1,2:T(8,128)(2,1)} copy(bf16[8,2,32,3456]{3,2,1,0:T(8,128)(2,1)S(1)} %reshape.61) | data formatting | bytes 7077888 | tf_op jit(solution)/shard_map/reshape | solution.py:58
  9.9 0.0 copy-start.1
  9.9 0.0 copy-start.2
  9.9 8.5 %all-to-all-start = ((bf16[8,2,32,3456]{3,0,1,2:T(8,128)(2,1)}), bf16[8,2,32,3456]{3,0,1,2:T(8,128)(2,1)}, u32[]{:S(2)}, u32[]{:S(2)}) async-start(bf16[8,2,32,3456]{3,0,1,2:T(8,128)(2,1)} %copy.13), calls=%async_computation | async-start | bytes 7077888 | tf_op jit(solution)/shard_map/all_to_all | solution.py:61
  18.5 0.0 copy-done.3
  18.5 0.6 dynamic-slice
  19.7 0.0 copy-done.1
  19.7 0.0 copy-done.2
  19.7 0.2 add_dynamic-update-slice_fusion
  19.9 52.5 %all-reduce = s32[512]{0:T(512)S(1)} all-reduce(s32[512]{0:T(512)S(1)} %add_dynamic-update-slice_fusion), channel_id=2, replica_groups=mesh['cls'=4,'dom'=32] {'dom'}, use_global_device_ids=true, to_apply=%add | all-reduce | flops 512 | bytes 4096
  72.4 0.1 reshape.54
  72.5 0.1 fusion.12
  72.5 0.1 eq.54
  72.6 0.1 eq.51
  72.7 2.5 %fusion.3 = f32[256,3456]{1,0:T(8,128)S(1)} fusion(f32[12,110592]{1,0:T(8,128)} %param.7, s32[]{:T(128)S(6)} %select_n.3, s32[256]{0:T(256)S(1)} %eq.54), kind=kOutput, calls=%fused_computation.5 | convolution fusion | flops 127405056 | bytes 3761156 | tf_op jit(solution)/shard_map/dot_general | solution.py:67
  75.3 2.0 %fusion.1 = f32[8,3456]{1,0:T(8,128)} fusion(f32[256,3456]{1,0:T(8,128)S(1)} %fusion.3, s32[256]{0:T(256)S(1)} %eq.51), kind=kOutput, calls=%fused_computation.2 | convolution fusion | flops 85821440 | bytes 3650560 | tf_op jit(solution)/shard_map/dot_general | solution.py:73
  77.3 1.6 %reshape.50 = f32[4,2,3456]{2,1,0:T(2,128)} reshape(f32[8,3456]{1,0:T(8,128)} %fusion.1) | data formatting | bytes 221184 | tf_op jit(solution)/shard_map/reshape | solution.py:75
  78.9 1.6 %copy.16 = f32[4,2,3456]{2,0,1:T(4,128)} copy(f32[4,2,3456]{2,1,0:T(2,128)} %reshape.50) | data formatting | bytes 221184 | tf_op jit(solution)/shard_map/reshape | solution.py:75
  80.4 0.0 all-to-all-done
  80.4 5.4 %fusion = f32[2,3456,256]{1,2,0:T(8,128)} fusion(bf16[8,2,32,3456]{3,0,1,2:T(8,128)(2,1)} %all-to-all-done, f32[256,3456]{1,0:T(8,128)S(1)} %fusion.3), kind=kLoop, calls=%fused_computation.1 | loop fusion | flops 3538944 | bytes 14155776 | tf_op jit(solution)/shard_map/kp,pcv->kcv/dot_general | solution.py:72
  85.8 8.0 %copy.15 = f32[2,3456,256]{2,1,0:T(8,128)} copy(f32[2,3456,256]{1,2,0:T(8,128)} %fusion) | data formatting | bytes 14155776 | tf_op jit(solution)/shard_map/kp,pcv->kcv/dot_general | solution.py:72
  93.8 0.0 copy-start
  93.8 6.3 %fusion.6 = f32[4,2,6912]{2,0,1:T(4,128)S(1)} fusion(f32[6912,256,1]{1,0,2:T(8,128)} %bitcast.23, s32[256]{0:T(256)S(1)} %eq.51, s32[4,2]{0,1:T(2,128)S(1)} %multiply_add_fusion), kind=kOutput, calls=%fused_computation.13 | convolution fusion | flops 169871360 | bytes 7300128 | tf_op jit(solution)/shard_map/kp,pcv->kcv/dot_general | solution.py:72
  100.1 0.0 copy-done
  100.1 0.1 maximum_bitcast_fusion
  100.2 0.2 copy.17
  100.4 11.3 %all_to_all.14 = f32[4,1,2,10368]{3,2,1,0:T(2,128)S(1)} all-to-all(f32[4,1,2,10368]{3,2,1,0:T(2,128)S(1)} %copy.17), channel_id=1, replica_groups=mesh['cls'=4,'dom'=32] {'cls'}, dimensions={0} | all-to-all | bytes 663552 | tf_op jit(solution)/shard_map/all_to_all | solution.py:34
  111.7 0.1 reduce_sum.11
  111.9 0.6 broadcast_add_fusion
  112.5 0.1 squeeze_reshape.3
  112.6 0.7 broadcast_divide_fusion
  (4 shorter events, 0.0 us)
Async XLA Ops:
  9.9 8.5 %copy-start.3 = (u32[128]{0:T(128)S(1)}, u32[128]{0:T(128)}, u32[]{:S(2)}) copy-start(u32[128]{0:T(128)} %constant.21) | copy-start | bytes 1540
  9.9 9.8 %copy-start.1 = (s32[8]{0:T(128)S(1)}, s32[8]{0:T(128)}, u32[]{:S(2)}) copy-start(s32[8]{0:T(128)} %param.6) | copy-start | bytes 100
  9.9 9.8 %copy-start.2 = (s32[8,1]{0,1:T(1,128)S(1)}, s32[8,1]{0,1:T(1,128)}, u32[]{:S(2)}) copy-start(s32[8,1]{0,1:T(1,128)} %param.5) | copy-start | bytes 100
  9.9 70.5 %all-to-all-start = ((bf16[8,2,32,3456]{3,0,1,2:T(8,128)(2,1)}), bf16[8,2,32,3456]{3,0,1,2:T(8,128)(2,1)}, u32[]{:S(2)}, u32[]{:S(2)}) async-start(bf16[8,2,32,3456]{3,0,1,2:T(8,128)(2,1)} %copy.13), calls=%async_computation | async-start | bytes 7077888 | tf_op jit(solution)/shard_map/all_to_all | solution.py:61
  93.8 6.3 %copy-start = (f32[4,2,3456]{2,0,1:T(4,128)S(1)}, f32[4,2,3456]{2,0,1:T(4,128)}, u32[]{:S(2)}) copy-start(f32[4,2,3456]{2,0,1:T(4,128)} %copy.16) | copy-start | bytes 331780
where the time goes:
time: 114 us; the launch traced here: 113 us
  blocking collectives  63.8 us (56%)
  local copies, waits for them, and re-layouts  21.7 us (19%)
  matrix products  10.8 us (9%)
  starting transfers between devices  8.52 us (7%)
  other arithmetic  7.07 us (6%)
  between operations  1.39 us (1%)
    unnamed x1, blocking collectives  52.5 us
    all_to_all x1, blocking collectives, summed_on_arrival(): lax.all_to_all(tiles, axis, split_axis=0, concat_axis=0, tiled=True)  11.3 us
    reshape x2, local copies, waits for them, and re-layouts, per_device(): parts_four = particles.reshape(p_dev, 2, n_dom, shard_len)  9.29 us
    all_to_all x1, starting transfers between devices, per_device(): lax.all_to_all(parts_four, 'dom', split_axis=2, concat_axis=0, tiled=True)  8.52 us
    dot_general x1, local copies, waits for them, and re-layouts, per_device(): jnp.einsum('kp,pcv->kcv', member, weighted, precision=lax.Precision.HIGHEST)  8.02 us
    dot_general x1, matrix products, per_device(): jnp.einsum('kp,pcv->kcv', member, weighted, precision=lax.Precision.HIGHEST)  6.29 us
    dot_general x1, other arithmetic, per_device(): jnp.einsum('kp,pcv->kcv', member, weighted, precision=lax.Precision.HIGHEST)  5.38 us
    reshape x2, local copies, waits for them, and re-layouts, per_device(): local_totals = local_totals.reshape(n_cls, CLS_GROUP, shard_len)  3.17 us
  transfers between devices with their start and end apart: 1, of which 0 were waited for; matrix products, arithmetic and copies ran while one was open for 8% of the time, Pallas kernels for 0%

commit v1 on v0

v1 whole, which is shorter than its diff:
```python
import functools

import jax
import jax.numpy as jnp
from jax import lax
from jax.experimental import pallas as pl
from jax.experimental.pallas import tpu as pltpu
from jax.sharding import PartitionSpec as P

F32 = jnp.float32
BF16 = jnp.bfloat16
MESH = pl.DeviceIdType.MESH
NB = 27
ROWS = 56
WEDGES = 12
PDEV = 8
PIECES = 16
HEAD = 40
TAIL = ROWS - HEAD
STREAM_ROWS = (HEAD, HEAD, 2 * TAIL)
N_COPIES = 21
WINDOW = 64


def kernel(lab, wed, x_hbm, table_hbm, avg_hbm, tot_hbm,
           xo, xp, fo, fp, tb, wexp, lab_p, wed_p, slot_p, slot_w,
           s0, s1, s2, r1_0, r1_1, r1_2, dp_0, dp_1, dp_2, dm_0, dm_1, dm_2,
           r2_0, r2_1, r2_2, ep_0, ep_1, ep_2, em_0, em_1, em_2,
           d3_0, d3_1, d3_2, oa, ow,
           sem_x, sem_t, sem_ps, sem_pr, sem_ls, sem_lr, sem_s, sem_r, sem_o):
    S = (s0, s1, s2)
    R1 = (r1_0, r1_1, r1_2)
    DP = (dp_0, dp_1, dp_2)
    DM = (dm_0, dm_1, dm_2)
    R2 = (r2_0, r2_1, r2_2)
    EP = (ep_0, ep_1, ep_2)
    EM = (em_0, em_1, em_2)
    D3 = (d3_0, d3_1, d3_2)
    y = lax.axis_index("cls")
    dom = lax.axis_index("dom")
    core = lax.rem(dom, 2)
    xc = lax.rem(dom // 2, 4)
    zc = dom // 8

    def device(dz=0, dx=0, dy=0, flip=False):
        c = 1 - core if flip else core
        zz, xx, yy = lax.rem(zc + dz, 4), lax.rem(xc + dx, 4), lax.rem(y + dy, 4)
        return (yy, (zz * 4 + xx) * 2 + c)

    def along(axis, step):
        return device(**{"d" + axis: step})

    partner = device(flip=True)
    AXES = (("x", "z", "y"), ("z", "y", "x"), ("y", "x", "z"))

    barrier = pltpu.get_barrier_semaphore()
    peers = [partner] + [along(a, s) for a in "xyz" for s in (1, 3, 2)]
    for peer in peers:
        pl.semaphore_signal(barrier, inc=1, device_id=peer, device_id_type=MESH)

    def shard_of(piece, c):
        dz, dx = piece // 4, lax.rem(piece, 4)
        return (lax.rem(zc + dz, 4) * 4 + lax.rem(xc + dx, 4)) * 2 + c

    def window(piece, c):
        row = shard_of(piece, c) * (2 * NB)
        start = jnp.minimum(row // 8, (64 * NB - WINDOW) // 8) * 8
        return pl.multiple_of(start, 8), row - start

    def own_copy(piece):
        start, _ = window(piece, core)
        return pltpu.make_async_copy(
            x_hbm.at[:, pl.ds(start, WINDOW)], xo.at[piece], sem_x.at[piece])

    def partner_copy(piece):
        start, _ = window(piece, 1 - core)
        return pltpu.make_async_remote_copy(
            src_ref=x_hbm.at[:, pl.ds(start, WINDOW)], dst_ref=xp.at[piece],
            send_sem=sem_ps.at[piece], recv_sem=sem_pr.at[piece],
            device_id=partner, device_id_type=MESH)

    def start_local(piece, carry):
        start = pl.multiple_of(shard_of(piece, core) * (NB * 128), 128)
        pltpu.make_async_copy(
            table_hbm.at[:, pl.ds(start, NB * 128)], tb.at[piece], sem_t).start()
        own_copy(piece).start()
        return carry

    lax.fori_loop(0, PIECES, start_local, 0)
    pl.semaphore_wait(barrier, len(peers))

    lab_copy = pltpu.make_async_remote_copy(
        src_ref=lab, dst_ref=lab_p, send_sem=sem_ls.at[0], recv_sem=sem_lr.at[0],
        device_id=partner, device_id_type=MESH)
    wed_copy = pltpu.make_async_remote_copy(
        src_ref=wed, dst_ref=wed_p, send_sem=sem_ls.at[1], recv_sem=sem_lr.at[1],
        device_id=partner, device_id_type=MESH)
    lab_copy.start()
    wed_copy.start()

    def start_partner(piece, carry):
        partner_copy(piece).start()
        return carry

    lax.fori_loop(0, PIECES, start_partner, 0)

    def slots(lab_ref, wed_ref, base):
        labels = [lab_ref[p] for p in range(PDEV)]
        wedges = [wed_ref[p] for p in range(PDEV)]

        def one_class(k, carry):
            p1, w1, p2, w2 = 0, WEDGES, 0, WEDGES
            seen = jnp.int32(0)
            for p in range(PDEV):
                hit = labels[p] == k
                first = hit & (seen == 0)
                second = hit & (seen > 0)
                p1 = jnp.where(first, p, p1)
                w1 = jnp.where(first, wedges[p], w1)
                p2 = jnp.where(second, p, p2)
                w2 = jnp.where(second, wedges[p], w2)
                seen = seen + hit.astype(jnp.int32)
            slot_p[k * 4 + base] = p1
            slot_w[k * 4 + base] = w1
            slot_p[k * 4 + base + 1] = p2
            slot_w[k * 4 + base + 1] = w2
            return carry

        lax.fori_loop(0, 8, one_class, 0)

    slots(lab, wed, 0)

    pltpu.make_async_copy(tb, tb, sem_t).wait()

    def expand(piece, carry):
        rows = wexp.at[piece].reshape((WEDGES + 1) * ROWS, 128)
        for b in range(NB):
            for lo, n in ((0, 8), (8, WEDGES - 8)):
                v = tb[piece, pl.ds(lo, n), pl.ds(b * 128, 128)]
                for c in range(2):
                    rows[pl.ds(lo * ROWS + 2 * b + c, n, stride=ROWS), :] = v
        wexp[piece, WEDGES] = jnp.zeros((ROWS, 128), F32)
        return carry

    lax.fori_loop(0, PIECES, expand, 0)

    sub = lax.broadcasted_iota(jnp.int32, (TAIL, 128), 0)
    lane = lax.broadcasted_iota(jnp.int32, (TAIL, 128), 1)

    def term(src, base, k, piece, lo, n):
        total = None
        for s in (base, base + 1):
            p = slot_p[k * 4 + s]
            w = slot_w[k * 4 + s]
            at = window(piece, core)[1]
            v = src[piece, p, pl.ds(at + lo, n), :] * wexp[piece, w, pl.ds(lo, n), :]
            total = v if total is None else total + v
        if lo + n == ROWS:
            count = jnp.zeros((n, 128), F32)
            for s in (base, base + 1):
                count = count + (lane == slot_w[k * 4 + s]).astype(F32)
            total = jnp.where(sub < TAIL - 2, total, jnp.where(sub == TAIL - 2, count, 0.0))
        return total

    def group(step):
        return lax.rem(y + step, 4) * 2

    def sums(stream, ra, rb, src, base, add):
        for rc in range(4):
            if stream == 0:
                parts = [(0, term(src, base, group(rc), rb * 4 + ra, 0, HEAD))]
            elif stream == 1:
                parts = [(0, term(src, base, group(rb) + 1, ra * 4 + rc, 0, HEAD))]
            else:
                parts = [(j * TAIL, term(src, base, group(ra) + j, rc * 4 + rb, HEAD, TAIL))
                         for j in range(2)]
            for at, v in parts:
                rows = pl.ds(at, v.shape[0])
                if add:
                    v = v + S[stream][ra, rb, rc, rows, :]
                S[stream][ra, rb, rc, rows, :] = v

    def unpack(src, dst, piece):
        def body(p, carry):
            dst[piece, p, pl.ds(0, WINDOW), :] = src[piece, p].astype(F32)
            return carry
        lax.fori_loop(0, PDEV, body, 0, unroll=True)

    def wait_own(piece, carry):
        own_copy(piece).wait()
        unpack(xo, fo, piece)
        return carry

    lax.fori_loop(0, PIECES, wait_own, 0)

    def own_pass(ra, carry):
        def inner(rb, c):
            for stream in range(3):
                sums(stream, ra, rb, fo, 0, False)
            return c
        return lax.fori_loop(0, 4, inner, carry)

    lax.fori_loop(0, 4, own_pass, 0)

    lab_copy.wait()
    wed_copy.wait()
    slots(lab_p, wed_p, 2)

    def wait_partner(piece, carry):
        partner_copy(piece).wait()
        unpack(xp, fp, piece)
        return carry

    lax.fori_loop(0, PIECES, wait_partner, 0)

    def copy(stream, i, src, dst, level, step):
        return pltpu.make_async_remote_copy(
            src_ref=src, dst_ref=dst, send_sem=sem_s.at[stream, i], recv_sem=sem_r.at[stream, i],
            device_id=along(AXES[stream][level], step), device_id_type=MESH)

    def relay1(t, rb):
        return copy(t, rb, S[t].at[2, rb], R1[t].at[rb], 0, 1 if rb >= 2 else 3)

    def own1(t, rb):
        if rb >= 2:
            return copy(t, 4 + rb, S[t].at[3, rb], DM[t].at[rb], 0, 3)
        return copy(t, 4 + rb, S[t].at[1, rb], DP[t].at[rb], 0, 1)

    def comb1(t, rb):
        if rb >= 2:
            return copy(t, 8 + rb, S[t].at[1, rb], DP[t].at[rb], 0, 1)
        return copy(t, 8 + rb, S[t].at[3, rb], DM[t].at[rb], 0, 3)

    HALF = (pl.ds(0, 2), pl.ds(2, 2))

    def relay2(t, h):
        return copy(t, 12 + h, S[t].at[0, 2, HALF[h]], R2[t].at[HALF[h]], 1, 1 if h else 3)

    def own2(t, h):
        if h:
            return copy(t, 14 + h, S[t].at[0, 3, HALF[h]], EM[t].at[HALF[h]], 1, 3)
        return copy(t, 14 + h, S[t].at[0, 1, HALF[h]], EP[t].at[HALF[h]], 1, 1)

    def comb2(t, h):
        if h:
            return copy(t, 16 + h, S[t].at[0, 1, HALF[h]], EP[t].at[HALF[h]], 1, 1)
        return copy(t, 16 + h, S[t].at[0, 3, HALF[h]], EM[t].at[HALF[h]], 1, 3)

    def last3(t, rc):
        return copy(t, 17 + rc, S[t].at[0, 0, rc], D3[t].at[rc - 1], 2, rc)

    started = []

    def go(c):
        c.start()
        started.append(c)

    for rb in (2, 1, 3, 0):
        for t in range(3):
            sums(t, 2, rb, fp, 2, True)
            go(relay1(t, rb))
    for rb in (1, 2, 0, 3):
        for t in range(3):
            sums(t, 1 if rb < 2 else 3, rb, fp, 2, True)
            go(own1(t, rb))
    for rb in (2, 1, 3, 0):
        for t in range(3):
            sums(t, 1 if rb >= 2 else 3, rb, fp, 2, True)

    def zero_pass(rb, carry):
        for t in range(3):
            sums(t, 0, rb, fp, 2, True)
        return carry

    lax.fori_loop(0, 4, zero_pass, 0)

    for rb in (2, 1, 3, 0):
        for t in range(3):
            relay1(t, rb).wait_recv()
            ra = 1 if rb >= 2 else 3
            S[t][ra, rb] = S[t][ra, rb] + R1[t][rb]
            go(comb1(t, rb))
    for rb in (2, 1, 3, 0):
        for t in range(3):
            own1(t, rb).wait_recv()
            comb1(t, rb).wait_recv()
            S[t][0, rb] = S[t][0, rb] + DP[t][rb] + DM[t][rb]
            if rb == 2:
                go(relay2(t, 0))
                go(relay2(t, 1))
            elif rb == 1:
                go(own2(t, 0))
                relay2(t, 1).wait_recv()
                S[t][0, 1, 2:4] = S[t][0, 1, 2:4] + R2[t][2:4]
                go(comb2(t, 1))
            elif rb == 3:
                go(own2(t, 1))
                relay2(t, 0).wait_recv()
                S[t][0, 3, 0:2] = S[t][0, 3, 0:2] + R2[t][0:2]
                go(comb2(t, 0))
    for t in range(3):
        for h in (1, 0):
            own2(t, h).wait_recv()
            comb2(t, h).wait_recv()
        S[t][0, 0] = S[t][0, 0] + EP[t][...] + EM[t][...]
        for rc in (2, 1, 3):
            go(last3(t, rc))
    final = []
    for t in (2, 0, 1):
        for rc in (1, 3, 2):
            last3(t, rc).wait_recv()
        final.append(S[t][0, 0, 0] + D3[t][0] + D3[t][1] + D3[t][2])
    tail, heads = final[0], final[1:]

    counts_lane = lax.broadcasted_iota(jnp.int32, (1, 128), 1)
    even = lax.rem(lax.broadcasted_iota(jnp.int32, (ROWS, 128), 0), 2) == 0
    totals = []
    for j in range(2):
        row = tail[j * TAIL + TAIL - 2:j * TAIL + TAIL - 1, :]
        total = jnp.zeros((ROWS, 128), F32)
        for w in range(WEDGES):
            n = jnp.sum(jnp.where(counts_lane == w, row, 0.0), axis=1, keepdims=True)
            a = wexp[0, w]
            total = total + n * (a * a)
        totals.append(total)
        summed = jnp.concatenate([heads[j], tail[j * TAIL:(j + 1) * TAIL]], axis=0)
        avg = summed / (total + 1.0)
        oa[j] = avg[0:2 * NB].reshape(NB, 2, 128)
    ow[...] = jnp.where(even, totals[0], totals[1])[0:2 * NB].reshape(NB, 2, 128)
    o1 = pltpu.make_async_copy(oa, avg_hbm, sem_o.at[0])
    o2 = pltpu.make_async_copy(ow, tot_hbm, sem_o.at[1])
    o1.start()
    o2.start()
    for c in started:
        c.wait_send()
    o1.wait()
    o2.wait()


def per_device(particles, labels, wedge_index, wedge_table):
    x = particles.reshape(PDEV, 2, 32 * NB, 128).transpose(0, 2, 1, 3)
    x = x.reshape(PDEV, 64 * NB, 128)
    lab = labels.reshape(PDEV)
    smem = pl.BlockSpec(memory_space=pltpu.SMEM)
    hbm = pl.BlockSpec(memory_space=pl.ANY)
    dma = pltpu.SemaphoreType.DMA
    V = pltpu.VMEM

    def per_stream(*lead):
        return [V((*lead, r, 128), F32) for r in STREAM_ROWS]

    avg, tot = pl.pallas_call(
        kernel,
        out_shape=(jax.ShapeDtypeStruct((2, NB, 2, 128), F32),
                   jax.ShapeDtypeStruct((NB, 2, 128), F32)),
        in_specs=[smem, smem, hbm, hbm],
        out_specs=(hbm, hbm),
        scratch_shapes=[
            V((PIECES, PDEV, WINDOW, 128), BF16),
            V((PIECES, PDEV, WINDOW, 128), BF16),
            V((PIECES, PDEV, WINDOW + 8, 128), F32),
            V((PIECES, PDEV, WINDOW + 8, 128), F32),
            V((PIECES, WEDGES, NB * 128), F32),
            V((PIECES, WEDGES + 1, ROWS, 128), F32),
            pltpu.SMEM((PDEV,), jnp.int32),
            pltpu.SMEM((PDEV,), jnp.int32),
            pltpu.SMEM((32,), jnp.int32),
            pltpu.SMEM((32,), jnp.int32),
            *per_stream(4, 4, 4),
            *per_stream(4, 4), *per_stream(4, 4), *per_stream(4, 4),
            *per_stream(4), *per_stream(4), *per_stream(4),
            *per_stream(3),
            V((2, NB, 2, 128), F32),
            V((NB, 2, 128), F32),
            dma((PIECES,)), dma(()), dma((PIECES,)), dma((PIECES,)), dma((2,)), dma((2,)),
            dma((3, N_COPIES)), dma((3, N_COPIES)), dma((2,)),
        ],
        compiler_params=pltpu.CompilerParams(
            collective_id=0, has_side_effects=True, vmem_limit_bytes=60 * 1024 * 1024),
        name="class_sums",
    )(lab, wedge_index, x, wedge_table)
    avg = avg.transpose(0, 2, 1, 3).reshape(2, 2, NB * 128)
    tot = tot.transpose(1, 0, 2).reshape(2, NB * 128)
    return avg, tot


def solution(mesh):
    return jax.shard_map(
        per_device,
        mesh=mesh,
        in_specs=(P(("cls", "dom"), None, None), P(("cls", "dom"), None), P(("cls", "dom")), P()),
        out_specs=(P("cls", None, "dom"), P("cls", "dom")),
        check_vma=False,
    )
```

time: 114 us -> 43.7 us (0.38)
  blocking collectives: 63.8 us -> 0 us
  Pallas kernels: 0 us -> 40.1 us
  local copies, waits for them, and re-layouts: 21.7 us -> 2.8 us
  matrix products: 10.8 us -> 0 us
  starting transfers between devices: 8.52 us -> 0 us
  other arithmetic: 7.07 us -> 0 us
    unnamed x1 -> x0, blocking collectives: 52.5 us -> none
    pallas_call x0 -> x1, Pallas kernels: none -> 40.1 us  [per_device(): pl.pallas_call(kernel, out_shape=(jax.ShapeDtypeStruct((2, NB, 2, 128), F...]
    reshape x5 -> x0, local copies, waits for them, and re-layouts: 12.6 us -> none  [the longest x2 9.29 us: per_device(): parts_four = particles.reshape(p_dev, 2, n_dom, shard_len)]
    all_to_all x1 -> x0, blocking collectives: 11.3 us -> none  [summed_on_arrival(): lax.all_to_all(tiles, axis, split_axis=0, concat_axis=0, tiled=True)]
    dot_general x3 -> x0, matrix products: 10.8 us -> none  [the longest x1 6.29 us: per_device(): jnp.einsum('kp,pcv->kcv', member, weighted, precision=lax.Precision.HIGHEST)]
    all_to_all x1 -> x0, starting transfers between devices: 8.52 us -> none  [per_device(): lax.all_to_all(parts_four, 'dom', split_axis=2, concat_axis=0, tiled=True)]
    dot_general x1 -> x0, local copies, waits for them, and re-layouts: 8.02 us -> none  [per_device(): jnp.einsum('kp,pcv->kcv', member, weighted, precision=lax.Precision.HIGHEST)]
    dot_general x1 -> x0, other arithmetic: 5.38 us -> none  [per_device(): jnp.einsum('kp,pcv->kcv', member, weighted, precision=lax.Precision.HIGHEST)]
  transfers between devices with their start and end apart: 1 -> 0, of which waited for: 0 -> 0; matrix products, arithmetic and copies ran while one was open for 8% -> 0% of each run, Pallas kernels for 0% -> 0%
where the time goes in v1:
time: 43.7 us; the launch traced here: 43.5 us
  Pallas kernels  40.1 us (92%)
  local copies, waits for them, and re-layouts  2.8 us (6%)
  between operations  0.64 us (1%)
    pallas_call x1, Pallas kernels, per_device(): pl.pallas_call(kernel, out_shape=(jax.ShapeDtypeStruct((2, NB, 2, 128), F...  40.1 us
    unnamed x2, local copies, waits for them, and re-layouts  2.8 us

profile of v1, /device:TPU:0, one launch (start us, length us, event | category | flops | bytes accessed | tf_op | source)
XLA Modules:
  0.0 43.5 jit_solution(11318678423105957225)
XLA Ops:
  0.6 40.1 %class_sums.1 = (f32[2,27,2,128]{3,2,1,0:T(2,128)}, f32[27,2,128]{2,1,0:T(2,128)}) custom-call(s32[8]{0:T(128)} %bitcast.15, s32[8]{0:T(128)} %wed.1, bf16[8,1728,128]{2,1,0:T(8,128)(2,1)} %bitcast.12, f32[12,110592]{1,0:T(8,128)} %table_hbm.1), custom_call_target="tpu_custom_call" | custom-call | tf_op jit(solution)/shard_map/class_sums/pallas_call | solution.py:352
  40.7 1.4 %copy.9 = f32[2,2,3456]{2,1,0:T(2,128)} copy(f32[2,2,3456]{2,1,0:T(2,128)} %bitcast.13) | data formatting | bytes 110592
  42.1 1.4 %copy.10 = f32[2,3456]{1,0:T(2,128)} copy(f32[2,3456]{1,0:T(2,128)} %bitcast.14) | data formatting | bytes 55296

commit v2 on v1

v2 whole, which is shorter than its diff:
```python
import jax
import jax.numpy as jnp
from jax import lax
from jax.experimental import pallas as pl
from jax.experimental.pallas import tpu as pltpu
from jax.sharding import PartitionSpec as P

F32 = jnp.float32
BF16 = jnp.bfloat16
MESH = pl.DeviceIdType.MESH
NB = 27
ROWS = 56
WEDGES = 12
PDEV = 8
PIECES = 16
HEAD = 40
TAIL = ROWS - HEAD
STREAM_ROWS = (HEAD, HEAD, 2 * TAIL)
N_COPIES = 21
WINDOW = 64
AXES = (("x", "z", "y"), ("z", "y", "x"), ("y", "x", "z"))
ORDER = ((2, 2), (3, 2), (1, 2), (0, 2), (2, 3), (2, 1), (2, 0), (3, 3),
         (1, 3), (0, 3), (1, 1), (0, 1), (3, 1), (1, 0), (3, 0), (0, 0))


def kernel(lab_hbm, wed_hbm, x_hbm, table_hbm, avg_ref, tot_ref,
           xo, xp, fo, fp, tb, wexp, lab, wed, lab_p, wed_p, slot_p, slot_w,
           s0, s1, s2, r1_0, r1_1, r1_2, dp_0, dp_1, dp_2, dm_0, dm_1, dm_2,
           r2_0, r2_1, r2_2, ep_0, ep_1, ep_2, em_0, em_1, em_2,
           d3_0, d3_1, d3_2,
           sem_x, sem_t, sem_l, sem_ps, sem_pr, sem_ls, sem_lr, sem_s, sem_r):
    S = (s0, s1, s2)
    R1 = (r1_0, r1_1, r1_2)
    DP = (dp_0, dp_1, dp_2)
    DM = (dm_0, dm_1, dm_2)
    R2 = (r2_0, r2_1, r2_2)
    EP = (ep_0, ep_1, ep_2)
    EM = (em_0, em_1, em_2)
    D3 = (d3_0, d3_1, d3_2)
    y = lax.axis_index("cls")
    dom = lax.axis_index("dom")
    core = lax.rem(dom, 2)
    xc = lax.rem(dom // 2, 4)
    zc = dom // 8

    def device(dz=0, dx=0, dy=0, flip=False):
        c = 1 - core if flip else core
        zz, xx, yy = lax.rem(zc + dz, 4), lax.rem(xc + dx, 4), lax.rem(y + dy, 4)
        return (yy, (zz * 4 + xx) * 2 + c)

    def along(axis, step):
        return device(**{"d" + axis: step})

    partner = device(flip=True)
    barrier = pltpu.get_barrier_semaphore()
    peers = [partner] + [along(a, s) for a in "xyz" for s in (1, 3, 2)]
    for peer in peers:
        pl.semaphore_signal(barrier, inc=1, device_id=peer, device_id_type=MESH)

    def shard_of(piece, c):
        dz, dx = piece // 4, piece % 4
        return (lax.rem(zc + dz, 4) * 4 + lax.rem(xc + dx, 4)) * 2 + c

    def window(piece, c):
        row = shard_of(piece, c) * (2 * NB)
        start = jnp.minimum(row // 8, (64 * NB - WINDOW) // 8) * 8
        return pl.multiple_of(start, 8), row - start

    def own_copy(piece):
        start, _ = window(piece, core)
        return pltpu.make_async_copy(
            x_hbm.at[:, pl.ds(start, WINDOW)], xo.at[piece], sem_x.at[piece])

    def table_copy(piece):
        start = pl.multiple_of(shard_of(piece, core) * (NB * 128), 128)
        return pltpu.make_async_copy(
            table_hbm.at[:, pl.ds(start, NB * 128)], tb.at[piece], sem_t.at[piece])

    def partner_copy(piece):
        start, _ = window(piece, 1 - core)
        return pltpu.make_async_remote_copy(
            src_ref=x_hbm.at[:, pl.ds(start, WINDOW)], dst_ref=xp.at[piece],
            send_sem=sem_ps.at[piece], recv_sem=sem_pr.at[piece],
            device_id=partner, device_id_type=MESH)

    order = [dz * 4 + dx for dz, dx in ORDER]
    lab_local = pltpu.make_async_copy(lab_hbm, lab, sem_l.at[0])
    wed_local = pltpu.make_async_copy(wed_hbm, wed, sem_l.at[1])
    lab_local.start()
    wed_local.start()
    for piece in order:
        table_copy(piece).start()
        own_copy(piece).start()
    pl.semaphore_wait(barrier, len(peers))

    lab_copy = pltpu.make_async_remote_copy(
        src_ref=lab_hbm, dst_ref=lab_p, send_sem=sem_ls.at[0], recv_sem=sem_lr.at[0],
        device_id=partner, device_id_type=MESH)
    wed_copy = pltpu.make_async_remote_copy(
        src_ref=wed_hbm, dst_ref=wed_p, send_sem=sem_ls.at[1], recv_sem=sem_lr.at[1],
        device_id=partner, device_id_type=MESH)
    lab_copy.start()
    wed_copy.start()
    for piece in order:
        partner_copy(piece).start()

    def slots(lab_ref, wed_ref, base):
        labels = [lab_ref[p] for p in range(PDEV)]
        wedges = [wed_ref[p] for p in range(PDEV)]

        def one_class(k, carry):
            p1, w1, p2, w2 = 0, WEDGES, 0, WEDGES
            seen = jnp.int32(0)
            for p in range(PDEV):
                hit = labels[p] == k
                first = hit & (seen == 0)
                second = hit & (seen > 0)
                p1 = jnp.where(first, p, p1)
                w1 = jnp.where(first, wedges[p], w1)
                p2 = jnp.where(second, p, p2)
                w2 = jnp.where(second, wedges[p], w2)
                seen = seen + hit.astype(jnp.int32)
            slot_p[k * 4 + base] = p1
            slot_w[k * 4 + base] = w1
            slot_p[k * 4 + base + 1] = p2
            slot_w[k * 4 + base + 1] = w2
            return carry

        lax.fori_loop(0, 8, one_class, 0)

    lab_local.wait()
    wed_local.wait()
    slots(lab, wed, 0)

    def expand(piece):
        rows = wexp.at[piece].reshape((WEDGES + 1) * ROWS, 128)
        for b in range(NB):
            for lo, n in ((0, 8), (8, WEDGES - 8)):
                v = tb[piece, pl.ds(lo, n), pl.ds(b * 128, 128)]
                for c in range(2):
                    rows[pl.ds(lo * ROWS + 2 * b + c, n, stride=ROWS), :] = v
        wexp[piece, WEDGES] = jnp.zeros((ROWS, 128), F32)

    def unpack(src, dst, piece):
        def body(p, carry):
            dst[piece, p, pl.ds(0, WINDOW), :] = src[piece, p].astype(F32)
            return carry
        lax.fori_loop(0, PDEV, body, 0, unroll=True)

    for piece in order:
        table_copy(piece).wait()
        own_copy(piece).wait()
        expand(piece)
        unpack(xo, fo, piece)

    lab_copy.wait()
    wed_copy.wait()
    slots(lab_p, wed_p, 2)

    sub = lax.broadcasted_iota(jnp.int32, (TAIL, 128), 0)
    lane = lax.broadcasted_iota(jnp.int32, (TAIL, 128), 1)

    def class_sum(dz, dx, at, dy, j):
        piece = dz * 4 + dx
        k = lax.rem(y + dy, 4) * 2 + j
        total = None
        count = jnp.zeros((TAIL, 128), F32)
        for s in range(4):
            p = slot_p[k * 4 + s]
            w = slot_w[k * 4 + s]
            src = fo if s < 2 else fp
            v = src[piece, p, pl.ds(at, ROWS), :] * wexp[piece, w]
            total = v if total is None else total + v
            count = count + (lane == w).astype(F32)
        tail = jnp.where(sub < TAIL - 2, total[HEAD:ROWS],
                         jnp.where(sub == TAIL - 2, count, 0.0))
        if j == 0:
            S[0][dx, dz, pl.ds(dy * HEAD, HEAD), :] = total[0:HEAD]
        else:
            S[1][dz, dy, pl.ds(dx * HEAD, HEAD), :] = total[0:HEAD]
        S[2][dy, dx, pl.ds(dz * 2 * TAIL + j * TAIL, TAIL), :] = tail

    def copy(stream, i, src, dst, level, step):
        return pltpu.make_async_remote_copy(
            src_ref=src, dst_ref=dst, send_sem=sem_s.at[stream, i], recv_sem=sem_r.at[stream, i],
            device_id=along(AXES[stream][level], step), device_id_type=MESH)

    def relay1(t, rb):
        return copy(t, rb, S[t].at[2, rb], R1[t].at[rb], 0, 1 if rb >= 2 else 3)

    def own1(t, rb):
        if rb >= 2:
            return copy(t, 4 + rb, S[t].at[3, rb], DM[t].at[rb], 0, 3)
        return copy(t, 4 + rb, S[t].at[1, rb], DP[t].at[rb], 0, 1)

    def comb1(t, rb):
        if rb >= 2:
            return copy(t, 8 + rb, S[t].at[1, rb], DP[t].at[rb], 0, 1)
        return copy(t, 8 + rb, S[t].at[3, rb], DM[t].at[rb], 0, 3)

    def half(t, h):
        n = 2 * STREAM_ROWS[t]
        return pl.ds(h * n, n)

    def relay2(t, h):
        return copy(t, 12 + h, S[t].at[0, 2, half(t, h)], R2[t].at[half(t, h)], 1, 1 if h else 3)

    def own2(t, h):
        if h:
            return copy(t, 14 + h, S[t].at[0, 3, half(t, h)], EM[t].at[half(t, h)], 1, 3)
        return copy(t, 14 + h, S[t].at[0, 1, half(t, h)], EP[t].at[half(t, h)], 1, 1)

    def comb2(t, h):
        if h:
            return copy(t, 16 + h, S[t].at[0, 1, half(t, h)], EP[t].at[half(t, h)], 1, 1)
        return copy(t, 16 + h, S[t].at[0, 3, half(t, h)], EM[t].at[half(t, h)], 1, 3)

    def last3(t, rc):
        n = STREAM_ROWS[t]
        return copy(t, 17 + rc, S[t].at[0, 0, pl.ds(rc * n, n)], D3[t].at[rc - 1], 2, rc)

    started = []

    def go(c):
        c.start()
        started.append(c)

    done = set()
    sent = set()
    sends = ([(0, relay1, rb, [(rb, 2)]) for rb in (2, 1, 3, 0)]
             + [(2, relay1, 2, [(d, 2) for d in range(4)])]
             + [(1, relay1, rb, [(2, d) for d in range(4)]) for rb in (2, 1, 3, 0)]
             + [(2, relay1, rb, [(d, rb) for d in range(4)]) for rb in (1, 3, 0)]
             + [(0, own1, rb, [(rb, 1 if rb < 2 else 3)]) for rb in (1, 2, 0, 3)]
             + [(1, own1, rb, [(1 if rb < 2 else 3, d) for d in range(4)]) for rb in (1, 2, 0, 3)]
             + [(2, own1, rb, [(d, rb) for d in range(4)]) for rb in (1, 2, 0, 3)])
    for dz, dx in ORDER:
        piece = dz * 4 + dx
        partner_copy(piece).wait()
        unpack(xp, fp, piece)
        at = window(piece, core)[1]

        def classes(dy, carry):
            for j in range(2):
                class_sum(dz, dx, at, dy, j)
            return carry

        lax.fori_loop(0, 4, classes, 0)
        done.add((dz, dx))
        for i, (t, make, rb, needs) in enumerate(sends):
            if i not in sent and done.issuperset(needs):
                sent.add(i)
                go(make(t, rb))

    for rb in (2, 1, 3, 0):
        for t in range(3):
            relay1(t, rb).wait_recv()
            ra = 1 if rb >= 2 else 3
            S[t][ra, rb] = S[t][ra, rb] + R1[t][rb]
            go(comb1(t, rb))
    for rb in (2, 1, 3, 0):
        for t in range(3):
            own1(t, rb).wait_recv()
            comb1(t, rb).wait_recv()
            S[t][0, rb] = S[t][0, rb] + DP[t][rb] + DM[t][rb]
            if rb == 2:
                go(relay2(t, 0))
                go(relay2(t, 1))
            elif rb == 1:
                go(own2(t, 0))
            elif rb == 3:
                go(own2(t, 1))
    for t in range(3):
        for h in (1, 0):
            relay2(t, h).wait_recv()
            rb = 1 if h else 3
            S[t][0, rb, half(t, h)] = S[t][0, rb, half(t, h)] + R2[t][half(t, h)]
            go(comb2(t, h))
    for t in range(3):
        for h in (1, 0):
            own2(t, h).wait_recv()
            comb2(t, h).wait_recv()
        S[t][0, 0] = S[t][0, 0] + EP[t][...] + EM[t][...]
        for rc in (2, 1, 3):
            go(last3(t, rc))
    final = []
    for t in (2, 0, 1):
        for rc in (1, 3, 2):
            last3(t, rc).wait_recv()
        final.append(S[t][0, 0, pl.ds(0, STREAM_ROWS[t])] + D3[t][0] + D3[t][1] + D3[t][2])
    tail, heads = final[0], final[1:]

    counts_lane = lax.broadcasted_iota(jnp.int32, (1, 128), 1)
    even = lax.rem(lax.broadcasted_iota(jnp.int32, (ROWS, 128), 0), 2) == 0
    totals = []
    for j in range(2):
        row = tail[j * TAIL + TAIL - 2:j * TAIL + TAIL - 1, :]
        total = jnp.zeros((ROWS, 128), F32)
        for w in range(WEDGES):
            n = jnp.sum(jnp.where(counts_lane == w, row, 0.0), axis=1, keepdims=True)
            a = wexp[0, w]
            total = total + n * (a * a)
        totals.append(total)
        summed = jnp.concatenate([heads[j], tail[j * TAIL:(j + 1) * TAIL]], axis=0)
        avg = summed / (total + 1.0)
        avg_ref[j] = avg[0:2 * NB].reshape(NB, 2, 128)
    tot_ref[...] = jnp.where(even, totals[0], totals[1])[0:2 * NB].reshape(NB, 2, 128)
    for c in started:
        c.wait_send()


def put_out(avg_ref, tot_ref, avg_out, tot_out, sems):
    one = pltpu.make_async_copy(avg_ref, avg_out, sems.at[0])
    two = pltpu.make_async_copy(tot_ref, tot_out, sems.at[1])
    one.start()
    two.start()
    one.wait()
    two.wait()


def per_device(particles, labels, wedge_index, wedge_table):
    x = particles.reshape(PDEV, 2, 32 * NB, 128).transpose(0, 2, 1, 3)
    x = x.reshape(PDEV, 64 * NB, 128)
    lab = labels.reshape(PDEV)
    hbm = pl.BlockSpec(memory_space=pltpu.HBM)
    vmem = pl.BlockSpec(memory_space=pltpu.VMEM)
    dma = pltpu.SemaphoreType.DMA
    V = pltpu.VMEM

    def per_stream(*lead, n=1):
        return [V((*lead, n * r, 128), F32) for r in STREAM_ROWS]

    shapes = (jax.ShapeDtypeStruct((2, NB, 2, 128), F32),
              jax.ShapeDtypeStruct((NB, 2, 128), F32))
    avg, tot = pl.pallas_call(
        kernel,
        out_shape=shapes,
        in_specs=[hbm] * 4,
        out_specs=(vmem, vmem),
        scratch_shapes=[
            V((PIECES, PDEV, WINDOW, 128), BF16),
            V((PIECES, PDEV, WINDOW, 128), BF16),
            V((PIECES, PDEV, WINDOW + 8, 128), F32),
            V((PIECES, PDEV, WINDOW + 8, 128), F32),
            V((PIECES, WEDGES, NB * 128), F32),
            V((PIECES, WEDGES + 1, ROWS, 128), F32),
            *[pltpu.SMEM((PDEV,), jnp.int32)] * 4,
            pltpu.SMEM((32,), jnp.int32),
            pltpu.SMEM((32,), jnp.int32),
            *per_stream(4, 4, n=4),
            *per_stream(4, n=4), *per_stream(4, n=4), *per_stream(4, n=4),
            *per_stream(n=4), *per_stream(n=4), *per_stream(n=4),
            *per_stream(3),
            dma((PIECES,)), dma((PIECES,)), dma((2,)), dma((PIECES,)), dma((PIECES,)),
            dma((2,)), dma((2,)), dma((3, N_COPIES)), dma((3, N_COPIES)),
        ],
        compiler_params=pltpu.CompilerParams(
            collective_id=0, has_side_effects=True, vmem_limit_bytes=44 * 1024 * 1024),
        name="class_sums",
    )(*[pltpu.with_memory_space_constraint(a, pltpu.HBM) for a in (lab, wedge_index, x, wedge_table)])
    avg, tot = pl.pallas_call(
        put_out,
        out_shape=shapes,
        in_specs=[vmem] * 2,
        out_specs=(hbm, hbm),
        scratch_shapes=[dma((2,))],
        compiler_params=pltpu.CompilerParams(vmem_limit_bytes=1024 * 1024),
        name="put_out",
    )(avg, tot)
    avg = avg.transpose(0, 2, 1, 3).reshape(2, 2, NB * 128)
    tot = tot.transpose(1, 0, 2).reshape(2, NB * 128)
    return avg, tot


def solution(mesh):
    return jax.shard_map(
        per_device,
        mesh=mesh,
        in_specs=(P(("cls", "dom"), None, None), P(("cls", "dom"), None), P(("cls", "dom")), P()),
        out_specs=(P("cls", None, "dom"), P("cls", "dom")),
        check_vma=False,
    )
```

time: 43.7 us -> 35.9 us (0.82)
  Pallas kernels: 40.1 us -> 35.1 us
  local copies, waits for them, and re-layouts: 2.8 us -> 0 us
    pallas_call x1 -> x2, Pallas kernels: 40.1 us -> 35.1 us  [the longest x1 34.5 us: per_device(): pl.pallas_call(kernel, out_shape=shapes, in_specs=[hbm] * 4, out_specs=(v...]
    unnamed x2 -> x0, local copies, waits for them, and re-layouts: 2.8 us -> none
where the time goes in v2:
time: 35.9 us; the launch traced here: 35.8 us
  Pallas kernels  35.1 us (98%)
  between operations  0.64 us (2%)
    pallas_call x1, Pallas kernels, per_device(): pl.pallas_call(kernel, out_shape=shapes, in_specs=[hbm] * 4, out_specs=(v...  34.5 us

profile of v2, /device:TPU:0, one launch (start us, length us, event | category | flops | bytes accessed | tf_op | source)
XLA Modules:
  0.0 35.8 jit_solution(17562652911955133307)
XLA Ops:
  0.6 34.5 %class_sums.1 = (f32[2,27,2,128]{3,2,1,0:T(2,128)S(1)}, f32[27,2,128]{2,1,0:T(2,128)S(1)}) custom-call(s32[8]{0:T(128)} %bitcast.13, s32[8]{0:T(128)} %wed_hbm.1, bf16[8,1728,128]{2,1,0:T(8,128)(2,1)} %bitcast.12, f32[12,110592]{1,0:T(8,128)} %table_hbm.1), custom_call_target="tpu_custom_call" | custom-call | tf_op jit(solution)/shard_map/class_sums/pallas_call | solution.py:335
  35.1 0.6 %put_out.1 = (f32[2,27,2,128]{3,2,1,0:T(2,128)}, f32[27,2,128]{2,1,0:T(2,128)}) custom-call(f32[2,27,2,128]{3,2,1,0:T(2,128)S(1)} %get-tuple-element.6.avg_ref, f32[27,2,128]{2,1,0:T(2,128)S(1)} %get-tuple-element.7.tot_ref), custom_call_target="tpu_custom_call" | custom-call | tf_op jit(solution)/shard_map/put_out/pallas_call | solution.py:361

commit v3 on v2

--- a/solution.py
+++ b/solution.py
@@ -18,6 +18,9 @@
 STREAM_ROWS = (HEAD, HEAD, 2 * TAIL)
 N_COPIES = 21
 WINDOW = 64
+TOP = 32700.0
+STEPS = 64.0
+LN2 = 0.6931471805599453
 AXES = (("x", "z", "y"), ("z", "y", "x"), ("y", "x", "z"))
 ORDER = ((2, 2), (3, 2), (1, 2), (0, 2), (2, 3), (2, 1), (2, 0), (3, 3),
          (1, 3), (0, 3), (1, 1), (0, 1), (3, 1), (1, 0), (3, 0), (0, 0))
@@ -25,14 +28,15 @@
 
 def kernel(lab_hbm, wed_hbm, x_hbm, table_hbm, avg_ref, tot_ref,
            xo, xp, fo, fp, tb, wexp, lab, wed, lab_p, wed_p, slot_p, slot_w,
-           s0, s1, s2, r1_0, r1_1, r1_2, dp_0, dp_1, dp_2, dm_0, dm_1, dm_2,
+           s0, s1, s2, qs_0, qs_1, qs_2, q1_0, q1_1, q1_2, qp_0, qp_1, qp_2, qm_0, qm_1, qm_2,
            r2_0, r2_1, r2_2, ep_0, ep_1, ep_2, em_0, em_1, em_2,
            d3_0, d3_1, d3_2,
            sem_x, sem_t, sem_l, sem_ps, sem_pr, sem_ls, sem_lr, sem_s, sem_r):
     S = (s0, s1, s2)
-    R1 = (r1_0, r1_1, r1_2)
-    DP = (dp_0, dp_1, dp_2)
-    DM = (dm_0, dm_1, dm_2)
+    QS = (qs_0, qs_1, qs_2)
+    Q1 = (q1_0, q1_1, q1_2)
+    QP = (qp_0, qp_1, qp_2)
+    QM = (qm_0, qm_1, qm_2)
     R2 = (r2_0, r2_1, r2_2)
     EP = (ep_0, ep_1, ep_2)
     EM = (em_0, em_1, em_2)
@@ -158,22 +162,45 @@
     slots(lab_p, wed_p, 2)
 
     sub = lax.broadcasted_iota(jnp.int32, (TAIL, 128), 0)
-    lane = lax.broadcasted_iota(jnp.int32, (TAIL, 128), 1)
+    sub8 = lax.broadcasted_iota(jnp.int32, (8, 128), 0)
+    lane8 = lax.broadcasted_iota(jnp.int32, (8, 128), 1)
+
+    def chip_counts(dy):
+        total = jnp.zeros((8, 128), F32)
+        for j in range(2):
+            k = lax.rem(y + dy, 4) * 2 + j
+            for s in range(4):
+                total = total + ((lane8 == slot_w[k * 4 + s]) & (sub8 == j)).astype(F32)
+        return total
+
+    def encode(t, dst, v, counts):
+        n = 4 * STREAM_ROWS[t]
+        v = v.reshape(n // 8, 8, 128)
+        top = jnp.maximum(jnp.max(jnp.abs(v), axis=0), 1e-30)
+        code = jnp.ceil(jnp.log(top) * (STEPS / LN2))
+        q = jnp.round(v * (jnp.exp(code * (-LN2 / STEPS)) * TOP)[None])
+        dst[pl.ds(0, n), :] = q.reshape(n, 128).astype(jnp.int32).astype(jnp.int16)
+        extra = jnp.concatenate([code, counts], axis=0)
+        dst[pl.ds(n, 16), :] = extra.astype(jnp.int32).astype(jnp.int16)
+
+    def decode(t, src):
+        n = 4 * STREAM_ROWS[t]
+        q = src[pl.ds(0, n), :].astype(jnp.int32).astype(F32)
+        extra = src[pl.ds(n, 16), :].astype(jnp.int32).astype(F32)
+        scale = jnp.exp(extra[0:8] * (LN2 / STEPS)) * (1.0 / TOP)
+        return (q.reshape(n // 8, 8, 128) * scale[None]).reshape(n, 128), extra[8:16]
 
     def class_sum(dz, dx, at, dy, j):
         piece = dz * 4 + dx
         k = lax.rem(y + dy, 4) * 2 + j
         total = None
-        count = jnp.zeros((TAIL, 128), F32)
         for s in range(4):
             p = slot_p[k * 4 + s]
             w = slot_w[k * 4 + s]
             src = fo if s < 2 else fp
             v = src[piece, p, pl.ds(at, ROWS), :] * wexp[piece, w]
             total = v if total is None else total + v
-            count = count + (lane == w).astype(F32)
-        tail = jnp.where(sub < TAIL - 2, total[HEAD:ROWS],
-                         jnp.where(sub == TAIL - 2, count, 0.0))
+        tail = jnp.where(sub < TAIL - 2, total[HEAD:ROWS], 0.0)
         if j == 0:
             S[0][dx, dz, pl.ds(dy * HEAD, HEAD), :] = total[0:HEAD]
         else:
@@ -186,17 +213,22 @@
             device_id=along(AXES[stream][level], step), device_id_type=MESH)
 
     def relay1(t, rb):
-        return copy(t, rb, S[t].at[2, rb], R1[t].at[rb], 0, 1 if rb >= 2 else 3)
+        return copy(t, rb, QS[t].at[rb], Q1[t].at[rb], 0, 1 if rb >= 2 else 3)
 
     def own1(t, rb):
         if rb >= 2:
-            return copy(t, 4 + rb, S[t].at[3, rb], DM[t].at[rb], 0, 3)
-        return copy(t, 4 + rb, S[t].at[1, rb], DP[t].at[rb], 0, 1)
+            return copy(t, 4 + rb, QS[t].at[4 + rb], QM[t].at[rb], 0, 3)
+        return copy(t, 4 + rb, QS[t].at[4 + rb], QP[t].at[rb], 0, 1)
 
     def comb1(t, rb):
         if rb >= 2:
-            return copy(t, 8 + rb, S[t].at[1, rb], DP[t].at[rb], 0, 1)
-        return copy(t, 8 + rb, S[t].at[3, rb], DM[t].at[rb], 0, 3)
+            return copy(t, 8 + rb, QS[t].at[8 + rb], QP[t].at[rb], 0, 1)
+        return copy(t, 8 + rb, QS[t].at[8 + rb], QM[t].at[rb], 0, 3)
+
+    none = jnp.zeros((8, 128), F32)
+
+    def counts_of(t, ra):
+        return chip_counts(ra) if t == 2 else none
 
     def half(t, h):
         n = 2 * STREAM_ROWS[t]
@@ -219,6 +251,8 @@
         n = STREAM_ROWS[t]
         return copy(t, 17 + rc, S[t].at[0, 0, pl.ds(rc * n, n)], D3[t].at[rc - 1], 2, rc)
 
+    row = lax.broadcasted_iota(jnp.int32, (8 * TAIL, 128), 0)
+    count_rows = [lax.rem(row, 2 * TAIL) == j * TAIL + TAIL - 2 for j in range(2)]
     started = []
 
     def go(c):
@@ -250,19 +284,31 @@
         for i, (t, make, rb, needs) in enumerate(sends):
             if i not in sent and done.issuperset(needs):
                 sent.add(i)
+                ra = 2 if make is relay1 else (3 if rb >= 2 else 1)
+                place = rb if make is relay1 else 4 + rb
+                encode(t, QS[t].at[place], S[t][ra, rb], counts_of(t, ra))
                 go(make(t, rb))
 
     for rb in (2, 1, 3, 0):
         for t in range(3):
             relay1(t, rb).wait_recv()
             ra = 1 if rb >= 2 else 3
-            S[t][ra, rb] = S[t][ra, rb] + R1[t][rb]
+            v, c = decode(t, Q1[t].at[rb])
+            encode(t, QS[t].at[8 + rb], S[t][ra, rb] + v, counts_of(t, ra) + c)
             go(comb1(t, rb))
     for rb in (2, 1, 3, 0):
         for t in range(3):
             own1(t, rb).wait_recv()
             comb1(t, rb).wait_recv()
-            S[t][0, rb] = S[t][0, rb] + DP[t][rb] + DM[t][rb]
+            vp, cp = decode(t, QP[t].at[rb])
+            vm, cm = decode(t, QM[t].at[rb])
+            total = S[t][0, rb] + vp + vm
+            if t == 2:
+                if rb == 2:
+                    ring_counts = chip_counts(0) + cp + cm
+                for j in range(2):
+                    total = total + jnp.where(count_rows[j], ring_counts[j:j + 1], 0.0)
+            S[t][0, rb] = total
             if rb == 2:
                 go(relay2(t, 0))
                 go(relay2(t, 1))
@@ -330,6 +376,9 @@
     def per_stream(*lead, n=1):
         return [V((*lead, n * r, 128), F32) for r in STREAM_ROWS]
 
+    def coded(n):
+        return [V((n, 4 * r + 16, 128), jnp.int16) for r in STREAM_ROWS]
+
     shapes = (jax.ShapeDtypeStruct((2, NB, 2, 128), F32),
               jax.ShapeDtypeStruct((NB, 2, 128), F32))
     avg, tot = pl.pallas_call(
@@ -348,7 +397,7 @@
             pltpu.SMEM((32,), jnp.int32),
             pltpu.SMEM((32,), jnp.int32),
             *per_stream(4, 4, n=4),
-            *per_stream(4, n=4), *per_stream(4, n=4), *per_stream(4, n=4),
+            *coded(12), *coded(4), *coded(4), *coded(4),
             *per_stream(n=4), *per_stream(n=4), *per_stream(n=4),
             *per_stream(3),
             dma((PIECES,)), dma((PIECES,)), dma((2,)), dma((PIECES,)), dma((PIECES,)),

time: 35.9 us -> 31.7 us (0.88)
  Pallas kernels: 35.1 us -> 30.9 us
    pallas_call x1, Pallas kernels: 34.5 us -> 30.2 us  [per_device(): pl.pallas_call(kernel, out_shape=shapes, in_specs=[hbm] * 4, out_specs=(v...]
where the time goes in v3:
time: 31.7 us; the launch traced here: 31.5 us
  Pallas kernels  30.9 us (97%)
  between operations  0.64 us (2%)
    pallas_call x1, Pallas kernels, per_device(): pl.pallas_call(kernel, out_shape=shapes, in_specs=[hbm] * 4, out_specs=(v...  30.2 us
    pallas_call x1, Pallas kernels, per_device(): pl.pallas_call(put_out, out_shape=shapes, in_specs=[vmem] * 2, out_specs=...  0.65 us

profile of v3, /device:TPU:0, one launch (start us, length us, event | category | flops | bytes accessed | tf_op | source)
XLA Modules:
  0.0 31.5 jit_solution(877622041097192864)
XLA Ops:
  0.6 30.2 %class_sums.1 = (f32[2,27,2,128]{3,2,1,0:T(2,128)S(1)}, f32[27,2,128]{2,1,0:T(2,128)S(1)}) custom-call(s32[8]{0:T(128)} %bitcast.13, s32[8]{0:T(128)} %wed_hbm.1, bf16[8,1728,128]{2,1,0:T(8,128)(2,1)} %bitcast.12, f32[12,110592]{1,0:T(8,128)} %table_hbm.1), custom_call_target="tpu_custom_call" | custom-call | tf_op jit(solution)/shard_map/class_sums/pallas_call | solution.py:384
  30.9 0.6 %put_out.1 = (f32[2,27,2,128]{3,2,1,0:T(2,128)}, f32[27,2,128]{2,1,0:T(2,128)}) custom-call(f32[2,27,2,128]{3,2,1,0:T(2,128)S(1)} %get-tuple-element.6.avg_ref, f32[27,2,128]{2,1,0:T(2,128)S(1)} %get-tuple-element.7.tot_ref), custom_call_target="tpu_custom_call" | custom-call | tf_op jit(solution)/shard_map/put_out/pallas_call | solution.py:410

commit v4 on v3

--- a/solution.py
+++ b/solution.py
@@ -16,7 +16,6 @@
 HEAD = 40
 TAIL = ROWS - HEAD
 STREAM_ROWS = (HEAD, HEAD, 2 * TAIL)
-N_COPIES = 21
 WINDOW = 64
 TOP = 32700.0
 STEPS = 64.0
@@ -28,19 +27,16 @@
 
 def kernel(lab_hbm, wed_hbm, x_hbm, table_hbm, avg_ref, tot_ref,
            xo, xp, fo, fp, tb, wexp, lab, wed, lab_p, wed_p, slot_p, slot_w,
-           s0, s1, s2, qs_0, qs_1, qs_2, q1_0, q1_1, q1_2, qp_0, qp_1, qp_2, qm_0, qm_1, qm_2,
-           r2_0, r2_1, r2_2, ep_0, ep_1, ep_2, em_0, em_1, em_2,
-           d3_0, d3_1, d3_2,
-           sem_x, sem_t, sem_l, sem_ps, sem_pr, sem_ls, sem_lr, sem_s, sem_r):
+           s0, s1, s2, qs_0, qs_1, qs_2, q1_0, q1_1, q1_2, qd_0, qd_1, qd_2,
+           qt_0, qt_1, qt_2, qf_0, qf_1, qf_2,
+           sem_x, sem_t, sem_l, sem_ps, sem_pr, sem_ls, sem_lr,
+           sem_s1, sem_s2, sem_r1, sem_rd, sem_rf):
     S = (s0, s1, s2)
     QS = (qs_0, qs_1, qs_2)
     Q1 = (q1_0, q1_1, q1_2)
-    QP = (qp_0, qp_1, qp_2)
-    QM = (qm_0, qm_1, qm_2)
-    R2 = (r2_0, r2_1, r2_2)
-    EP = (ep_0, ep_1, ep_2)
-    EM = (em_0, em_1, em_2)
-    D3 = (d3_0, d3_1, d3_2)
+    QD = (qd_0, qd_1, qd_2)
+    QT = (qt_0, qt_1, qt_2)
+    QF = (qf_0, qf_1, qf_2)
     y = lax.axis_index("cls")
     dom = lax.axis_index("dom")
     core = lax.rem(dom, 2)
@@ -61,40 +57,45 @@
     for peer in peers:
         pl.semaphore_signal(barrier, inc=1, device_id=peer, device_id_type=MESH)
 
-    def shard_of(piece, c):
-        dz, dx = piece // 4, piece % 4
+    def shard_of(pos, c):
+        dz, dx = ORDER[pos]
         return (lax.rem(zc + dz, 4) * 4 + lax.rem(xc + dx, 4)) * 2 + c
 
-    def window(piece, c):
-        row = shard_of(piece, c) * (2 * NB)
+    def window(pos, c):
+        row = shard_of(pos, c) * (2 * NB)
         start = jnp.minimum(row // 8, (64 * NB - WINDOW) // 8) * 8
         return pl.multiple_of(start, 8), row - start
 
-    def own_copy(piece):
-        start, _ = window(piece, core)
+    def own_copy(pos):
+        start, _ = window(pos, core)
         return pltpu.make_async_copy(
-            x_hbm.at[:, pl.ds(start, WINDOW)], xo.at[piece], sem_x.at[piece])
-
-    def table_copy(piece):
-        start = pl.multiple_of(shard_of(piece, core) * (NB * 128), 128)
+            x_hbm.at[:, pl.ds(start, WINDOW)], xo.at[pos], sem_x.at[pos // 4])
+
+    def table_copy(pos):
+        start = pl.multiple_of(shard_of(pos, core) * (NB * 128), 128)
         return pltpu.make_async_copy(
-            table_hbm.at[:, pl.ds(start, NB * 128)], tb.at[piece], sem_t.at[piece])
-
-    def partner_copy(piece):
-        start, _ = window(piece, 1 - core)
+            table_hbm.at[:, pl.ds(start, NB * 128)], tb.at[pos], sem_t.at[pos // 4])
+
+    def batch_of(pos):
+        return (pos + 2) // 3
+
+    def partner_copy(pos):
+        start, _ = window(pos, 1 - core)
         return pltpu.make_async_remote_copy(
-            src_ref=x_hbm.at[:, pl.ds(start, WINDOW)], dst_ref=xp.at[piece],
-            send_sem=sem_ps.at[piece], recv_sem=sem_pr.at[piece],
+            src_ref=x_hbm.at[:, pl.ds(start, WINDOW)], dst_ref=xp.at[pos],
+            send_sem=sem_ps, recv_sem=sem_pr.at[batch_of(pos)],
             device_id=partner, device_id_type=MESH)
 
-    order = [dz * 4 + dx for dz, dx in ORDER]
+    def wait_bytes(ref, sem):
+        pltpu.make_async_copy(ref, ref, sem).wait()
+
     lab_local = pltpu.make_async_copy(lab_hbm, lab, sem_l.at[0])
     wed_local = pltpu.make_async_copy(wed_hbm, wed, sem_l.at[1])
     lab_local.start()
     wed_local.start()
-    for piece in order:
-        table_copy(piece).start()
-        own_copy(piece).start()
+    for pos in range(PIECES):
+        table_copy(pos).start()
+        own_copy(pos).start()
     pl.semaphore_wait(barrier, len(peers))
 
     lab_copy = pltpu.make_async_remote_copy(
@@ -105,8 +106,8 @@
         device_id=partner, device_id_type=MESH)
     lab_copy.start()
     wed_copy.start()
-    for piece in order:
-        partner_copy(piece).start()
+    for pos in range(PIECES):
+        partner_copy(pos).start()
 
     def slots(lab_ref, wed_ref, base):
         labels = [lab_ref[p] for p in range(PDEV)]
@@ -151,14 +152,15 @@
             return carry
         lax.fori_loop(0, PDEV, body, 0, unroll=True)
 
-    for piece in order:
-        table_copy(piece).wait()
-        own_copy(piece).wait()
-        expand(piece)
-        unpack(xo, fo, piece)
-
-    lab_copy.wait()
-    wed_copy.wait()
+    for pos in range(PIECES):
+        if pos % 4 == 0:
+            wait_bytes(tb.at[pl.ds(pos, 4)], sem_t.at[pos // 4])
+            wait_bytes(xo.at[pl.ds(pos, 4)], sem_x.at[pos // 4])
+        expand(pos)
+        unpack(xo, fo, pos)
+
+    lab_copy.wait_recv()
+    wed_copy.wait_recv()
     slots(lab_p, wed_p, 2)
 
     sub = lax.broadcasted_iota(jnp.int32, (TAIL, 128), 0)
@@ -173,25 +175,22 @@
                 total = total + ((lane8 == slot_w[k * 4 + s]) & (sub8 == j)).astype(F32)
         return total
 
-    def encode(t, dst, v, counts):
-        n = 4 * STREAM_ROWS[t]
+    def encode(dst, v, *more):
+        n = v.shape[0]
         v = v.reshape(n // 8, 8, 128)
         top = jnp.maximum(jnp.max(jnp.abs(v), axis=0), 1e-30)
         code = jnp.ceil(jnp.log(top) * (STEPS / LN2))
         q = jnp.round(v * (jnp.exp(code * (-LN2 / STEPS)) * TOP)[None])
-        dst[pl.ds(0, n), :] = q.reshape(n, 128).astype(jnp.int32).astype(jnp.int16)
-        extra = jnp.concatenate([code, counts], axis=0)
-        dst[pl.ds(n, 16), :] = extra.astype(jnp.int32).astype(jnp.int16)
-
-    def decode(t, src):
-        n = 4 * STREAM_ROWS[t]
-        q = src[pl.ds(0, n), :].astype(jnp.int32).astype(F32)
-        extra = src[pl.ds(n, 16), :].astype(jnp.int32).astype(F32)
-        scale = jnp.exp(extra[0:8] * (LN2 / STEPS)) * (1.0 / TOP)
-        return (q.reshape(n // 8, 8, 128) * scale[None]).reshape(n, 128), extra[8:16]
-
-    def class_sum(dz, dx, at, dy, j):
-        piece = dz * 4 + dx
+        rows = jnp.concatenate([q.reshape(n, 128), code, *more], axis=0)
+        dst[...] = rows.astype(jnp.int32).astype(jnp.int16)
+
+    def decode(src, n):
+        rows = src[...].astype(jnp.int32).astype(F32)
+        scale = jnp.exp(rows[n:n + 8] * (LN2 / STEPS)) * (1.0 / TOP)
+        return (rows[0:n].reshape(n // 8, 8, 128) * scale[None]).reshape(n, 128), rows[n + 8:]
+
+    def class_sum(piece, at, dy, j):
+        dz, dx = ORDER[piece]
         k = lax.rem(y + dy, 4) * 2 + j
         total = None
         for s in range(4):
@@ -207,23 +206,29 @@
             S[1][dz, dy, pl.ds(dx * HEAD, HEAD), :] = total[0:HEAD]
         S[2][dy, dx, pl.ds(dz * 2 * TAIL + j * TAIL, TAIL), :] = tail
 
-    def copy(stream, i, src, dst, level, step):
+    def ring(t, src, dst, recv, step):
         return pltpu.make_async_remote_copy(
-            src_ref=src, dst_ref=dst, send_sem=sem_s.at[stream, i], recv_sem=sem_r.at[stream, i],
-            device_id=along(AXES[stream][level], step), device_id_type=MESH)
+            src_ref=src, dst_ref=dst, send_sem=sem_s1.at[t], recv_sem=recv,
+            device_id=along(AXES[t][0], step), device_id_type=MESH)
 
     def relay1(t, rb):
-        return copy(t, rb, QS[t].at[rb], Q1[t].at[rb], 0, 1 if rb >= 2 else 3)
+        return ring(t, QS[t].at[rb], Q1[t].at[rb], sem_r1.at[t, rb], 1 if rb >= 2 else 3)
 
     def own1(t, rb):
-        if rb >= 2:
-            return copy(t, 4 + rb, QS[t].at[4 + rb], QM[t].at[rb], 0, 3)
-        return copy(t, 4 + rb, QS[t].at[4 + rb], QP[t].at[rb], 0, 1)
+        side = 1 if rb >= 2 else 0
+        return ring(t, QS[t].at[4 + rb], QD[t].at[rb, side], sem_rd.at[t, rb], 3 if side else 1)
 
     def comb1(t, rb):
-        if rb >= 2:
-            return copy(t, 8 + rb, QS[t].at[8 + rb], QP[t].at[rb], 0, 1)
-        return copy(t, 8 + rb, QS[t].at[8 + rb], QM[t].at[rb], 0, 3)
+        side = 0 if rb >= 2 else 1
+        return ring(t, QS[t].at[8 + rb], QD[t].at[rb, side], sem_rd.at[t, rb], 3 if side else 1)
+
+    def plane(t, rb, rc):
+        m = rb * 4 + rc - 1
+        target = device(**{"d" + AXES[t][1]: rb, "d" + AXES[t][2]: rc})
+        return pltpu.make_async_remote_copy(
+            src_ref=QT[t].at[m], dst_ref=QF[t].at[m],
+            send_sem=sem_s2.at[t], recv_sem=sem_rf.at[t],
+            device_id=target, device_id_type=MESH)
 
     none = jnp.zeros((8, 128), F32)
 
@@ -250,14 +255,6 @@
     def last3(t, rc):
         n = STREAM_ROWS[t]
         return copy(t, 17 + rc, S[t].at[0, 0, pl.ds(rc * n, n)], D3[t].at[rc - 1], 2, rc)
-
-    row = lax.broadcasted_iota(jnp.int32, (8 * TAIL, 128), 0)
-    count_rows = [lax.rem(row, 2 * TAIL) == j * TAIL + TAIL - 2 for j in range(2)]
-    started = []
-
-    def go(c):
-        c.start()
-        started.append(c)
 
     done = set()
     sent = set()
@@ -268,91 +265,90 @@
              + [(0, own1, rb, [(rb, 1 if rb < 2 else 3)]) for rb in (1, 2, 0, 3)]
              + [(1, own1, rb, [(1 if rb < 2 else 3, d) for d in range(4)]) for rb in (1, 2, 0, 3)]
              + [(2, own1, rb, [(d, rb) for d in range(4)]) for rb in (1, 2, 0, 3)])
-    for dz, dx in ORDER:
-        piece = dz * 4 + dx
-        partner_copy(piece).wait()
-        unpack(xp, fp, piece)
-        at = window(piece, core)[1]
+    for pos in range(PIECES):
+        if pos == 0 or batch_of(pos) != batch_of(pos - 1):
+            batch = [p for p in range(PIECES) if batch_of(p) == batch_of(pos)]
+            wait_bytes(xp.at[pl.ds(pos, len(batch))], sem_pr.at[batch_of(pos)])
+        unpack(xp, fp, pos)
+        at = window(pos, core)[1]
 
         def classes(dy, carry):
             for j in range(2):
-                class_sum(dz, dx, at, dy, j)
+                class_sum(pos, at, dy, j)
             return carry
 
         lax.fori_loop(0, 4, classes, 0)
-        done.add((dz, dx))
+        done.add(ORDER[pos])
         for i, (t, make, rb, needs) in enumerate(sends):
             if i not in sent and done.issuperset(needs):
                 sent.add(i)
                 ra = 2 if make is relay1 else (3 if rb >= 2 else 1)
                 place = rb if make is relay1 else 4 + rb
-                encode(t, QS[t].at[place], S[t][ra, rb], counts_of(t, ra))
-                go(make(t, rb))
+                encode(QS[t].at[place], S[t][ra, rb], counts_of(t, ra))
+                make(t, rb).start()
 
     for rb in (2, 1, 3, 0):
         for t in range(3):
+            n = 4 * STREAM_ROWS[t]
             relay1(t, rb).wait_recv()
             ra = 1 if rb >= 2 else 3
-            v, c = decode(t, Q1[t].at[rb])
-            encode(t, QS[t].at[8 + rb], S[t][ra, rb] + v, counts_of(t, ra) + c)
-            go(comb1(t, rb))
+            v, c = decode(Q1[t].at[rb], n)
+            encode(QS[t].at[8 + rb], S[t][ra, rb] + v, counts_of(t, ra) + c)
+            comb1(t, rb).start()
+    kept = [None] * 3
     for rb in (2, 1, 3, 0):
         for t in range(3):
-            own1(t, rb).wait_recv()
-            comb1(t, rb).wait_recv()
-            vp, cp = decode(t, QP[t].at[rb])
-            vm, cm = decode(t, QM[t].at[rb])
-            total = S[t][0, rb] + vp + vm
+            wait_bytes(QD[t].at[rb], sem_rd.at[t, rb])
+        for t in range(3):
+            r = STREAM_ROWS[t]
+            v0, c0 = decode(QD[t].at[rb, 0], 4 * r)
+            v1, c1 = decode(QD[t].at[rb, 1], 4 * r)
+            total = S[t][0, rb] + v0 + v1
+            more = ()
             if t == 2:
                 if rb == 2:
-                    ring_counts = chip_counts(0) + cp + cm
-                for j in range(2):
-                    total = total + jnp.where(count_rows[j], ring_counts[j:j + 1], 0.0)
-            S[t][0, rb] = total
-            if rb == 2:
-                go(relay2(t, 0))
-                go(relay2(t, 1))
-            elif rb == 1:
-                go(own2(t, 0))
-            elif rb == 3:
-                go(own2(t, 1))
-    for t in range(3):
-        for h in (1, 0):
-            relay2(t, h).wait_recv()
-            rb = 1 if h else 3
-            S[t][0, rb, half(t, h)] = S[t][0, rb, half(t, h)] + R2[t][half(t, h)]
-            go(comb2(t, h))
-    for t in range(3):
-        for h in (1, 0):
-            own2(t, h).wait_recv()
-            comb2(t, h).wait_recv()
-        S[t][0, 0] = S[t][0, 0] + EP[t][...] + EM[t][...]
-        for rc in (2, 1, 3):
-            go(last3(t, rc))
+                    counts = chip_counts(0) + c0 + c1
+                more = (counts,)
+            for rc in (2, 1, 3, 0):
+                part = total[rc * r:(rc + 1) * r]
+                if rb or rc:
+                    encode(QT[t].at[rb * 4 + rc - 1], part, *more)
+                    plane(t, rb, rc).start()
+                else:
+                    kept[t] = part
     final = []
     for t in (2, 0, 1):
-        for rc in (1, 3, 2):
-            last3(t, rc).wait_recv()
-        final.append(S[t][0, 0, pl.ds(0, STREAM_ROWS[t])] + D3[t][0] + D3[t][1] + D3[t][2])
+        wait_bytes(QF[t], sem_rf.at[t])
+        total = kept[t]
+        for m in range(15):
+            v, c = decode(QF[t].at[m], STREAM_ROWS[t])
+            total = total + v
+            if t == 2:
+                counts = counts + c
+        final.append(total)
     tail, heads = final[0], final[1:]
 
     counts_lane = lax.broadcasted_iota(jnp.int32, (1, 128), 1)
     even = lax.rem(lax.broadcasted_iota(jnp.int32, (ROWS, 128), 0), 2) == 0
     totals = []
     for j in range(2):
-        row = tail[j * TAIL + TAIL - 2:j * TAIL + TAIL - 1, :]
+        row = counts[j:j + 1]
         total = jnp.zeros((ROWS, 128), F32)
         for w in range(WEDGES):
             n = jnp.sum(jnp.where(counts_lane == w, row, 0.0), axis=1, keepdims=True)
-            a = wexp[0, w]
+            a = wexp[PIECES - 1, w]
             total = total + n * (a * a)
         totals.append(total)
         summed = jnp.concatenate([heads[j], tail[j * TAIL:(j + 1) * TAIL]], axis=0)
         avg = summed / (total + 1.0)
         avg_ref[j] = avg[0:2 * NB].reshape(NB, 2, 128)
     tot_ref[...] = jnp.where(even, totals[0], totals[1])[0:2 * NB].reshape(NB, 2, 128)
-    for c in started:
-        c.wait_send()
+    for t in range(3):
+        wait_bytes(QS[t], sem_s1.at[t])
+        wait_bytes(QT[t], sem_s2.at[t])
+    wait_bytes(xp, sem_ps)
+    lab_copy.wait_send()
+    wed_copy.wait_send()
 
 
 def put_out(avg_ref, tot_ref, avg_out, tot_out, sems):
@@ -373,11 +369,11 @@
     dma = pltpu.SemaphoreType.DMA
     V = pltpu.VMEM
 
-    def per_stream(*lead, n=1):
-        return [V((*lead, n * r, 128), F32) for r in STREAM_ROWS]
-
-    def coded(n):
-        return [V((n, 4 * r + 16, 128), jnp.int16) for r in STREAM_ROWS]
+    def per_stream(*lead):
+        return [V((*lead, 4 * r, 128), F32) for r in STREAM_ROWS]
+
+    def coded(*lead):
+        return [V((*lead, 4 * r + 16, 128), jnp.int16) for r in STREAM_ROWS]
 
     shapes = (jax.ShapeDtypeStruct((2, NB, 2, 128), F32),
               jax.ShapeDtypeStruct((NB, 2, 128), F32))
@@ -396,12 +392,11 @@
             *[pltpu.SMEM((PDEV,), jnp.int32)] * 4,
             pltpu.SMEM((32,), jnp.int32),
             pltpu.SMEM((32,), jnp.int32),
-            *per_stream(4, 4, n=4),
-            *coded(12), *coded(4), *coded(4), *coded(4),
-            *per_stream(n=4), *per_stream(n=4), *per_stream(n=4),
-            *per_stream(3),
-            dma((PIECES,)), dma((PIECES,)), dma((2,)), dma((PIECES,)), dma((PIECES,)),
-            dma((2,)), dma((2,)), dma((3, N_COPIES)), dma((3, N_COPIES)),
+            *per_stream(4, 4),
+            *coded(12), *coded(4), *coded(4, 2),
+            *[V((15, HEAD + 8, 128), jnp.int16)] * 6,
+            dma((4,)), dma((4,)), dma((2,)), dma(()), dma((6,)), dma((2,)), dma((2,)),
+            dma((3,)), dma((3,)), dma((3, 4)), dma((3, 4)), dma((3,)),
         ],
         compiler_params=pltpu.CompilerParams(
             collective_id=0, has_side_effects=True, vmem_limit_bytes=44 * 1024 * 1024),

time: 31.7 us -> 27.2 us (0.86); the launches traced: 31.5 us -> 26.7 us
  Pallas kernels: 30.9 us -> 26.1 us
    pallas_call x1, Pallas kernels: 30.2 us -> 25.4 us  [per_device(): pl.pallas_call(kernel, out_shape=shapes, in_specs=[hbm] * 4, out_specs=(v...]
where the time goes in v4:
time: 27.2 us; the launch traced here: 26.7 us
  Pallas kernels  26.1 us (96%)
  between operations  0.64 us (2%)
    pallas_call x1, Pallas kernels, per_device(): pl.pallas_call(kernel, out_shape=shapes, in_specs=[hbm] * 4, out_specs=(v...  25.4 us
    pallas_call x1, Pallas kernels, per_device(): pl.pallas_call(put_out, out_shape=shapes, in_specs=[vmem] * 2, out_specs=...  0.65 us

profile of v4, /device:TPU:0, one launch (start us, length us, event | category | flops | bytes accessed | tf_op | source)
XLA Modules:
  0.0 26.7 jit_solution(1707678288516399755)
XLA Ops:
  0.6 25.4 %class_sums.1 = (f32[2,27,2,128]{3,2,1,0:T(2,128)S(1)}, f32[27,2,128]{2,1,0:T(2,128)S(1)}) custom-call(s32[8]{0:T(128)} %bitcast.13, s32[8]{0:T(128)} %wed_hbm.1, bf16[8,1728,128]{2,1,0:T(8,128)(2,1)} %bitcast.12, f32[12,110592]{1,0:T(8,128)} %table_hbm.1), custom_call_target="tpu_custom_call" | custom-call | tf_op jit(solution)/shard_map/class_sums/pallas_call | solution.py:380
  26.0 0.6 %put_out.1 = (f32[2,27,2,128]{3,2,1,0:T(2,128)}, f32[27,2,128]{2,1,0:T(2,128)}) custom-call(f32[2,27,2,128]{3,2,1,0:T(2,128)S(1)} %get-tuple-element.6.avg_ref, f32[27,2,128]{2,1,0:T(2,128)S(1)} %get-tuple-element.7.tot_ref), custom_call_target="tpu_custom_call" | custom-call | tf_op jit(solution)/shard_map/put_out/pallas_call | solution.py:405

commit v5 on v4

--- a/solution.py
+++ b/solution.py
@@ -20,9 +20,11 @@
 TOP = 32700.0
 STEPS = 64.0
 LN2 = 0.6931471805599453
-AXES = (("x", "z", "y"), ("z", "y", "x"), ("y", "x", "z"))
-ORDER = ((2, 2), (3, 2), (1, 2), (0, 2), (2, 3), (2, 1), (2, 0), (3, 3),
-         (1, 3), (0, 3), (1, 1), (0, 1), (3, 1), (1, 0), (3, 0), (0, 0))
+AXES = (("x", "z", "y"), ("z", "x", "y"), ("y", "x", "z"))
+ORDER = ((2, 2), (1, 2), (2, 1), (3, 2), (2, 3), (0, 2), (2, 0), (1, 1),
+         (0, 1), (3, 1), (3, 3), (1, 3), (0, 3), (1, 0), (3, 0), (0, 0))
+BATCH = (0, 1, 2, 3, 4, 5, 5, 6, 6, 6, 7, 7, 7, 8, 8, 8)
+DIRECT = ((2, 3), (2, 0))
 
 
 def kernel(lab_hbm, wed_hbm, x_hbm, table_hbm, avg_ref, tot_ref,
@@ -77,7 +79,7 @@
             table_hbm.at[:, pl.ds(start, NB * 128)], tb.at[pos], sem_t.at[pos // 4])
 
     def batch_of(pos):
-        return (pos + 2) // 3
+        return BATCH[pos]
 
     def partner_copy(pos):
         start, _ = window(pos, 1 - core)
@@ -203,7 +205,7 @@
         if j == 0:
             S[0][dx, dz, pl.ds(dy * HEAD, HEAD), :] = total[0:HEAD]
         else:
-            S[1][dz, dy, pl.ds(dx * HEAD, HEAD), :] = total[0:HEAD]
+            S[1][dz, dx, pl.ds(dy * HEAD, HEAD), :] = total[0:HEAD]
         S[2][dy, dx, pl.ds(dz * 2 * TAIL + j * TAIL, TAIL), :] = tail
 
     def ring(t, src, dst, recv, step):
@@ -211,7 +213,9 @@
             src_ref=src, dst_ref=dst, send_sem=sem_s1.at[t], recv_sem=recv,
             device_id=along(AXES[t][0], step), device_id_type=MESH)
 
-    def relay1(t, rb):
+    def far1(t, rb):
+        if (t, rb) in DIRECT:
+            return ring(t, QS[t].at[rb], QD[t].at[rb, 2], sem_rd.at[t, rb], 2)
         return ring(t, QS[t].at[rb], Q1[t].at[rb], sem_r1.at[t, rb], 1 if rb >= 2 else 3)
 
     def own1(t, rb):
@@ -221,6 +225,9 @@
     def comb1(t, rb):
         side = 0 if rb >= 2 else 1
         return ring(t, QS[t].at[8 + rb], QD[t].at[rb, side], sem_rd.at[t, rb], 3 if side else 1)
+
+    def arrivals(t, rb):
+        return 3 if (t, rb) in DIRECT else 2
 
     def plane(t, rb, rc):
         m = rb * 4 + rc - 1
@@ -258,13 +265,16 @@
 
     done = set()
     sent = set()
-    sends = ([(0, relay1, rb, [(rb, 2)]) for rb in (2, 1, 3, 0)]
-             + [(2, relay1, 2, [(d, 2) for d in range(4)])]
-             + [(1, relay1, rb, [(2, d) for d in range(4)]) for rb in (2, 1, 3, 0)]
-             + [(2, relay1, rb, [(d, rb) for d in range(4)]) for rb in (1, 3, 0)]
-             + [(0, own1, rb, [(rb, 1 if rb < 2 else 3)]) for rb in (1, 2, 0, 3)]
-             + [(1, own1, rb, [(1 if rb < 2 else 3, d) for d in range(4)]) for rb in (1, 2, 0, 3)]
-             + [(2, own1, rb, [(d, rb) for d in range(4)]) for rb in (1, 2, 0, 3)])
+    def column(rb):
+        return [(d, rb) for d in range(4)]
+
+    sends = ([(0, far1, rb, rb, 2, [(rb, 2)]) for rb in (2, 1, 3, 0)]
+             + [(1, far1, rb, rb, 2, [(2, rb)]) for rb in (2, 1, 3, 0)]
+             + [(2, far1, rb, rb, 2, column(rb)) for rb in (2, 1, 3, 0)]
+             + [(0, own1, 4 + rb, rb, ra, [(rb, ra)]) for rb, ra in ((1, 1), (2, 3), (0, 1), (3, 3))]
+             + [(1, own1, 4 + rb, rb, ra, [(ra, rb)]) for rb, ra in ((1, 1), (2, 3), (0, 1), (3, 3))]
+             + [(2, own1, 4 + rb, rb, ra, column(rb)) for rb, ra in ((1, 1), (2, 3), (0, 1), (3, 3))]
+             + [(t, comb1, 8 + rb, rb, 1 if rb >= 2 else 3, column(rb)) for t, rb in DIRECT])
     for pos in range(PIECES):
         if pos == 0 or batch_of(pos) != batch_of(pos - 1):
             batch = [p for p in range(PIECES) if batch_of(p) == batch_of(pos)]
@@ -279,45 +289,51 @@
 
         lax.fori_loop(0, 4, classes, 0)
         done.add(ORDER[pos])
-        for i, (t, make, rb, needs) in enumerate(sends):
+        for i, (t, make, place, rb, ra, needs) in enumerate(sends):
             if i not in sent and done.issuperset(needs):
                 sent.add(i)
-                ra = 2 if make is relay1 else (3 if rb >= 2 else 1)
-                place = rb if make is relay1 else 4 + rb
                 encode(QS[t].at[place], S[t][ra, rb], counts_of(t, ra))
                 make(t, rb).start()
 
-    for rb in (2, 1, 3, 0):
-        for t in range(3):
-            n = 4 * STREAM_ROWS[t]
-            relay1(t, rb).wait_recv()
-            ra = 1 if rb >= 2 else 3
-            v, c = decode(Q1[t].at[rb], n)
-            encode(QS[t].at[8 + rb], S[t][ra, rb] + v, counts_of(t, ra) + c)
-            comb1(t, rb).start()
+    for t, rb in ((0, 2), (1, 2), (0, 1), (1, 1), (2, 2), (0, 3), (1, 3), (0, 0), (1, 0), (2, 1)):
+        far1(t, rb).wait_recv()
+        ra = 1 if rb >= 2 else 3
+        v, c = decode(Q1[t].at[rb], 4 * STREAM_ROWS[t])
+        encode(QS[t].at[8 + rb], S[t][ra, rb] + v, counts_of(t, ra) + c)
+        comb1(t, rb).start()
     kept = [None] * 3
-    for rb in (2, 1, 3, 0):
-        for t in range(3):
-            wait_bytes(QD[t].at[rb], sem_rd.at[t, rb])
-        for t in range(3):
-            r = STREAM_ROWS[t]
-            v0, c0 = decode(QD[t].at[rb, 0], 4 * r)
-            v1, c1 = decode(QD[t].at[rb, 1], 4 * r)
-            total = S[t][0, rb] + v0 + v1
-            more = ()
+    waited = set()
+
+    def wait_ring(t, rb):
+        if (t, rb) not in waited:
+            waited.add((t, rb))
+            wait_bytes(QD[t].at[rb, pl.ds(0, arrivals(t, rb))], sem_rd.at[t, rb])
+
+    wait_ring(0, 2)
+    wait_ring(1, 2)
+    counts = None
+    for t, rb in ((0, 2), (1, 2), (2, 3), (0, 1), (1, 1), (0, 3), (1, 3), (0, 0), (2, 0), (1, 0), (2, 2), (2, 1)):
+        wait_ring(t, rb)
+        r = STREAM_ROWS[t]
+        total = S[t][0, rb]
+        seen = chip_counts(0) if t == 2 else None
+        for side in range(arrivals(t, rb)):
+            v, c = decode(QD[t].at[rb, side], 4 * r)
+            total = total + v
             if t == 2:
-                if rb == 2:
-                    counts = chip_counts(0) + c0 + c1
-                more = (counts,)
-            for rc in (2, 1, 3, 0):
-                part = total[rc * r:(rc + 1) * r]
-                if rb or rc:
-                    encode(QT[t].at[rb * 4 + rc - 1], part, *more)
-                    plane(t, rb, rc).start()
-                else:
-                    kept[t] = part
+                seen = seen + c
+        if t == 2 and counts is None:
+            counts = seen
+        more = (counts,) if t == 2 else ()
+        for rc in (2, 1, 3, 0):
+            part = total[rc * r:(rc + 1) * r]
+            if rb or rc:
+                encode(QT[t].at[rb * 4 + rc - 1], part, *more)
+                plane(t, rb, rc).start()
+            else:
+                kept[t] = part
     final = []
-    for t in (2, 0, 1):
+    for t in (0, 1, 2):
         wait_bytes(QF[t], sem_rf.at[t])
         total = kept[t]
         for m in range(15):
@@ -326,7 +342,7 @@
             if t == 2:
                 counts = counts + c
         final.append(total)
-    tail, heads = final[0], final[1:]
+    tail, heads = final[2], final[:2]
 
     counts_lane = lax.broadcasted_iota(jnp.int32, (1, 128), 1)
     even = lax.rem(lax.broadcasted_iota(jnp.int32, (ROWS, 128), 0), 2) == 0
@@ -393,9 +409,9 @@
             pltpu.SMEM((32,), jnp.int32),
             pltpu.SMEM((32,), jnp.int32),
             *per_stream(4, 4),
-            *coded(12), *coded(4), *coded(4, 2),
+            *coded(12), *coded(4), *coded(4, 3),
             *[V((15, HEAD + 8, 128), jnp.int16)] * 6,
-            dma((4,)), dma((4,)), dma((2,)), dma(()), dma((6,)), dma((2,)), dma((2,)),
+            dma((4,)), dma((4,)), dma((2,)), dma(()), dma((9,)), dma((2,)), dma((2,)),
             dma((3,)), dma((3,)), dma((3, 4)), dma((3, 4)), dma((3,)),
         ],
         compiler_params=pltpu.CompilerParams(

time: 27.2 us -> 26.3 us (0.967)
  the two profiles are of different devices: /device:TPU:0 before, /device:TPU:1 now
where the time goes in v5:
time: 26.3 us; the launch traced here: 26.1 us
  Pallas kernels  25.5 us (97%)
  between operations  0.64 us (2%)
    pallas_call x1, Pallas kernels, per_device(): pl.pallas_call(kernel, out_shape=shapes, in_specs=[hbm] * 4, out_specs=(v...  24.8 us
    pallas_call x1, Pallas kernels, per_device(): pl.pallas_call(put_out, out_shape=shapes, in_specs=[vmem] * 2, out_specs=...  0.65 us

profile of v5, /device:TPU:1, one launch (start us, length us, event | category | flops | bytes accessed | tf_op | source)
XLA Modules:
  0.0 26.1 jit_solution(5302970004770954687)
XLA Ops:
  0.6 24.8 %class_sums.1 = (f32[2,27,2,128]{3,2,1,0:T(2,128)S(1)}, f32[27,2,128]{2,1,0:T(2,128)S(1)}) custom-call(s32[8]{0:T(128)} %bitcast.13, s32[8]{0:T(128)} %wed_hbm.1, bf16[8,1728,128]{2,1,0:T(8,128)(2,1)} %bitcast.12, f32[12,110592]{1,0:T(8,128)} %table_hbm.1), custom_call_target="tpu_custom_call" | custom-call | tf_op jit(solution)/shard_map/class_sums/pallas_call | solution.py:396
  25.5 0.6 %put_out.1 = (f32[2,27,2,128]{3,2,1,0:T(2,128)}, f32[27,2,128]{2,1,0:T(2,128)}) custom-call(f32[2,27,2,128]{3,2,1,0:T(2,128)S(1)} %get-tuple-element.6.avg_ref, f32[27,2,128]{2,1,0:T(2,128)S(1)} %get-tuple-element.7.tot_ref), custom_call_target="tpu_custom_call" | custom-call | tf_op jit(solution)/shard_map/put_out/pallas_call | solution.py:421

commit v6 on v5

--- a/solution.py
+++ b/solution.py
@@ -17,6 +17,8 @@
 TAIL = ROWS - HEAD
 STREAM_ROWS = (HEAD, HEAD, 2 * TAIL)
 WINDOW = 64
+WROWS = 72
+EMPTY = 10000
 TOP = 32700.0
 STEPS = 64.0
 LN2 = 0.6931471805599453
@@ -24,11 +26,12 @@
 ORDER = ((2, 2), (1, 2), (2, 1), (3, 2), (2, 3), (0, 2), (2, 0), (1, 1),
          (0, 1), (3, 1), (3, 3), (1, 3), (0, 3), (1, 0), (3, 0), (0, 0))
 BATCH = (0, 1, 2, 3, 4, 5, 5, 6, 6, 6, 7, 7, 7, 8, 8, 8)
+HOLD = 7
 DIRECT = ((2, 3), (2, 0))
 
 
 def kernel(lab_hbm, wed_hbm, x_hbm, table_hbm, avg_ref, tot_ref,
-           xo, xp, fo, fp, tb, wexp, lab, wed, lab_p, wed_p, slot_p, slot_w,
+           xo, xp, prod, tb, wexp, lab, wed, lab_p, wed_p, slot_p, slot_w,
            s0, s1, s2, qs_0, qs_1, qs_2, q1_0, q1_1, q1_2, qd_0, qd_1, qd_2,
            qt_0, qt_1, qt_2, qf_0, qf_1, qf_2,
            sem_x, sem_t, sem_l, sem_ps, sem_pr, sem_ls, sem_lr,
@@ -116,15 +119,15 @@
         wedges = [wed_ref[p] for p in range(PDEV)]
 
         def one_class(k, carry):
-            p1, w1, p2, w2 = 0, WEDGES, 0, WEDGES
+            p1, w1, p2, w2 = EMPTY, WEDGES, EMPTY, WEDGES
             seen = jnp.int32(0)
             for p in range(PDEV):
                 hit = labels[p] == k
                 first = hit & (seen == 0)
                 second = hit & (seen > 0)
-                p1 = jnp.where(first, p, p1)
+                p1 = jnp.where(first, base * 4 + p, p1)
                 w1 = jnp.where(first, wedges[p], w1)
-                p2 = jnp.where(second, p, p2)
+                p2 = jnp.where(second, base * 4 + p, p2)
                 w2 = jnp.where(second, wedges[p], w2)
                 seen = seen + hit.astype(jnp.int32)
             slot_p[k * 4 + base] = p1
@@ -139,27 +142,28 @@
     wed_local.wait()
     slots(lab, wed, 0)
 
-    def expand(piece):
-        rows = wexp.at[piece].reshape((WEDGES + 1) * ROWS, 128)
+    def expand(pos):
+        rows = wexp.at[pos].reshape(WEDGES * WROWS, 128)
+        at = window(pos, core)[1]
         for b in range(NB):
             for lo, n in ((0, 8), (8, WEDGES - 8)):
-                v = tb[piece, pl.ds(lo, n), pl.ds(b * 128, 128)]
+                v = tb[pos, pl.ds(lo, n), pl.ds(b * 128, 128)]
                 for c in range(2):
-                    rows[pl.ds(lo * ROWS + 2 * b + c, n, stride=ROWS), :] = v
-        wexp[piece, WEDGES] = jnp.zeros((ROWS, 128), F32)
-
-    def unpack(src, dst, piece):
-        def body(p, carry):
-            dst[piece, p, pl.ds(0, WINDOW), :] = src[piece, p].astype(F32)
-            return carry
-        lax.fori_loop(0, PDEV, body, 0, unroll=True)
+                    rows[pl.ds(at + lo * WROWS + 2 * b + c, n, stride=WROWS), :] = v
+
+    def weigh(src, wedges, base, pos):
+        for p in range(PDEV):
+            prod[pos * 16 + base + p, pl.ds(0, WINDOW), :] = (
+                src[pos, p].astype(F32) * wexp[pos, wedges[p], pl.ds(0, WINDOW), :])
+
+    prod[PIECES * 16] = jnp.zeros((WROWS, 128), F32)
 
     for pos in range(PIECES):
         if pos % 4 == 0:
             wait_bytes(tb.at[pl.ds(pos, 4)], sem_t.at[pos // 4])
             wait_bytes(xo.at[pl.ds(pos, 4)], sem_x.at[pos // 4])
         expand(pos)
-        unpack(xo, fo, pos)
+        weigh(xo, wed, 0, pos)
 
     lab_copy.wait_recv()
     wed_copy.wait_recv()
@@ -196,10 +200,8 @@
         k = lax.rem(y + dy, 4) * 2 + j
         total = None
         for s in range(4):
-            p = slot_p[k * 4 + s]
-            w = slot_w[k * 4 + s]
-            src = fo if s < 2 else fp
-            v = src[piece, p, pl.ds(at, ROWS), :] * wexp[piece, w]
+            place = jnp.minimum(slot_p[k * 4 + s] + piece * 16, PIECES * 16)
+            v = prod[place, pl.ds(at, ROWS), :]
             total = v if total is None else total + v
         tail = jnp.where(sub < TAIL - 2, total[HEAD:ROWS], 0.0)
         if j == 0:
@@ -237,10 +239,8 @@
             send_sem=sem_s2.at[t], recv_sem=sem_rf.at[t],
             device_id=target, device_id_type=MESH)
 
-    none = jnp.zeros((8, 128), F32)
-
     def counts_of(t, ra):
-        return chip_counts(ra) if t == 2 else none
+        return (chip_counts(ra),) if t == 2 else ()
 
     def half(t, h):
         n = 2 * STREAM_ROWS[t]
@@ -264,6 +264,7 @@
         return copy(t, 17 + rc, S[t].at[0, 0, pl.ds(rc * n, n)], D3[t].at[rc - 1], 2, rc)
 
     done = set()
+    held = []
     sent = set()
     def column(rb):
         return [(d, rb) for d in range(4)]
@@ -279,7 +280,7 @@
         if pos == 0 or batch_of(pos) != batch_of(pos - 1):
             batch = [p for p in range(PIECES) if batch_of(p) == batch_of(pos)]
             wait_bytes(xp.at[pl.ds(pos, len(batch))], sem_pr.at[batch_of(pos)])
-        unpack(xp, fp, pos)
+        weigh(xp, wed_p, 8, pos)
         at = window(pos, core)[1]
 
         def classes(dy, carry):
@@ -292,14 +293,20 @@
         for i, (t, make, place, rb, ra, needs) in enumerate(sends):
             if i not in sent and done.issuperset(needs):
                 sent.add(i)
-                encode(QS[t].at[place], S[t][ra, rb], counts_of(t, ra))
-                make(t, rb).start()
-
-    for t, rb in ((0, 2), (1, 2), (0, 1), (1, 1), (2, 2), (0, 3), (1, 3), (0, 0), (1, 0), (2, 1)):
+                encode(QS[t].at[place], S[t][ra, rb], *counts_of(t, ra))
+                if make is own1 and pos < HOLD:
+                    held.append((t, rb))
+                else:
+                    make(t, rb).start()
+        if pos == HOLD:
+            for t, rb in held:
+                own1(t, rb).start()
+
+    for t, rb in ((0, 2), (1, 2), (0, 1), (1, 1), (0, 3), (2, 2), (1, 3), (0, 0), (1, 0), (2, 1)):
         far1(t, rb).wait_recv()
         ra = 1 if rb >= 2 else 3
         v, c = decode(Q1[t].at[rb], 4 * STREAM_ROWS[t])
-        encode(QS[t].at[8 + rb], S[t][ra, rb] + v, counts_of(t, ra) + c)
+        encode(QS[t].at[8 + rb], S[t][ra, rb] + v, *[n + c for n in counts_of(t, ra)])
         comb1(t, rb).start()
     kept = [None] * 3
     waited = set()
@@ -312,7 +319,7 @@
     wait_ring(0, 2)
     wait_ring(1, 2)
     counts = None
-    for t, rb in ((0, 2), (1, 2), (2, 3), (0, 1), (1, 1), (0, 3), (1, 3), (0, 0), (2, 0), (1, 0), (2, 2), (2, 1)):
+    for t, rb in ((0, 2), (1, 2), (2, 3), (0, 1), (1, 1), (2, 2), (2, 1), (0, 3), (1, 3), (0, 0), (2, 0), (1, 0)):
         wait_ring(t, rb)
         r = STREAM_ROWS[t]
         total = S[t][0, rb]
@@ -346,13 +353,14 @@
 
     counts_lane = lax.broadcasted_iota(jnp.int32, (1, 128), 1)
     even = lax.rem(lax.broadcasted_iota(jnp.int32, (ROWS, 128), 0), 2) == 0
+    own_at = window(PIECES - 1, core)[1]
     totals = []
     for j in range(2):
         row = counts[j:j + 1]
         total = jnp.zeros((ROWS, 128), F32)
         for w in range(WEDGES):
             n = jnp.sum(jnp.where(counts_lane == w, row, 0.0), axis=1, keepdims=True)
-            a = wexp[PIECES - 1, w]
+            a = wexp[PIECES - 1, w, pl.ds(own_at, ROWS), :]
             total = total + n * (a * a)
         totals.append(total)
         summed = jnp.concatenate([heads[j], tail[j * TAIL:(j + 1) * TAIL]], axis=0)
@@ -389,7 +397,8 @@
         return [V((*lead, 4 * r, 128), F32) for r in STREAM_ROWS]
 
     def coded(*lead):
-        return [V((*lead, 4 * r + 16, 128), jnp.int16) for r in STREAM_ROWS]
+        return [V((*lead, 4 * r + extra, 128), jnp.int16)
+                for r, extra in zip(STREAM_ROWS, (8, 8, 16))]
 
     shapes = (jax.ShapeDtypeStruct((2, NB, 2, 128), F32),
               jax.ShapeDtypeStruct((NB, 2, 128), F32))
@@ -401,10 +410,9 @@
         scratch_shapes=[
             V((PIECES, PDEV, WINDOW, 128), BF16),
             V((PIECES, PDEV, WINDOW, 128), BF16),
-            V((PIECES, PDEV, WINDOW + 8, 128), F32),
-            V((PIECES, PDEV, WINDOW + 8, 128), F32),
+            V((PIECES * 16 + 1, WROWS, 128), F32),
             V((PIECES, WEDGES, NB * 128), F32),
-            V((PIECES, WEDGES + 1, ROWS, 128), F32),
+            V((PIECES, WEDGES, WROWS, 128), F32),
             *[pltpu.SMEM((PDEV,), jnp.int32)] * 4,
             pltpu.SMEM((32,), jnp.int32),
             pltpu.SMEM((32,), jnp.int32),

time: 26.3 us -> 25.9 us (0.985)
  the two profiles are of different devices: /device:TPU:1 before, /device:TPU:0 now
where the time goes in v6:
time: 25.9 us; the launch traced here: 25.7 us
  Pallas kernels  25.1 us (97%)
  between operations  0.64 us (2%)
    pallas_call x1, Pallas kernels, per_device(): pl.pallas_call(kernel, out_shape=shapes, in_specs=[hbm] * 4, out_specs=(v...  24.4 us
    pallas_call x1, Pallas kernels, per_device(): pl.pallas_call(put_out, out_shape=shapes, in_specs=[vmem] * 2, out_specs=...  0.65 us

profile of v6, /device:TPU:0, one launch (start us, length us, event | category | flops | bytes accessed | tf_op | source)
XLA Modules:
  0.0 25.7 jit_solution(1210724953678927917)
XLA Ops:
  0.6 24.4 %class_sums.1 = (f32[2,27,2,128]{3,2,1,0:T(2,128)S(1)}, f32[27,2,128]{2,1,0:T(2,128)S(1)}) custom-call(s32[8]{0:T(128)} %bitcast.13, s32[8]{0:T(128)} %wed_hbm.1, bf16[8,1728,128]{2,1,0:T(8,128)(2,1)} %bitcast.12, f32[12,110592]{1,0:T(8,128)} %table_hbm.1), custom_call_target="tpu_custom_call" | custom-call | tf_op jit(solution)/shard_map/class_sums/pallas_call | solution.py:405
  25.1 0.6 %put_out.1 = (f32[2,27,2,128]{3,2,1,0:T(2,128)}, f32[27,2,128]{2,1,0:T(2,128)}) custom-call(f32[2,27,2,128]{3,2,1,0:T(2,128)S(1)} %get-tuple-element.6.avg_ref, f32[27,2,128]{2,1,0:T(2,128)S(1)} %get-tuple-element.7.tot_ref), custom_call_target="tpu_custom_call" | custom-call | tf_op jit(solution)/shard_map/put_out/pallas_call | solution.py:429

commit v7 on v6

--- a/solution.py
+++ b/solution.py
@@ -288,7 +288,7 @@
                 class_sum(pos, at, dy, j)
             return carry
 
-        lax.fori_loop(0, 4, classes, 0)
+        lax.fori_loop(0, 4, classes, 0, unroll=True)
         done.add(ORDER[pos])
         for i, (t, make, place, rb, ra, needs) in enumerate(sends):
             if i not in sent and done.issuperset(needs):

time: 25.9 us -> 25.6 us (0.988); the launches traced: 25.7 us -> 25.1 us
  Pallas kernels: 25.1 us -> 24.5 us
    pallas_call x1, Pallas kernels: 24.4 us -> 23.8 us  [per_device(): pl.pallas_call(kernel, out_shape=shapes, in_specs=[hbm] * 4, out_specs=(v...]
where the time goes in v7:
time: 25.6 us; the launch traced here: 25.1 us
  Pallas kernels  24.5 us (96%)
  between operations  0.64 us (2%)
    pallas_call x1, Pallas kernels, per_device(): pl.pallas_call(kernel, out_shape=shapes, in_specs=[hbm] * 4, out_specs=(v...  23.8 us
    pallas_call x1, Pallas kernels, per_device(): pl.pallas_call(put_out, out_shape=shapes, in_specs=[vmem] * 2, out_specs=...  0.65 us

profile of v7, /device:TPU:0, one launch (start us, length us, event | category | flops | bytes accessed | tf_op | source)
XLA Modules:
  0.0 25.1 jit_solution(14901526984280287484)
XLA Ops:
  0.6 23.8 %class_sums.1 = (f32[2,27,2,128]{3,2,1,0:T(2,128)S(1)}, f32[27,2,128]{2,1,0:T(2,128)S(1)}) custom-call(s32[8]{0:T(128)} %bitcast.13, s32[8]{0:T(128)} %wed_hbm.1, bf16[8,1728,128]{2,1,0:T(8,128)(2,1)} %bitcast.12, f32[12,110592]{1,0:T(8,128)} %table_hbm.1), custom_call_target="tpu_custom_call" | custom-call | tf_op jit(solution)/shard_map/class_sums/pallas_call | solution.py:405
  24.4 0.6 %put_out.1 = (f32[2,27,2,128]{3,2,1,0:T(2,128)}, f32[27,2,128]{2,1,0:T(2,128)}) custom-call(f32[2,27,2,128]{3,2,1,0:T(2,128)S(1)} %get-tuple-element.6.avg_ref, f32[27,2,128]{2,1,0:T(2,128)S(1)} %get-tuple-element.7.tot_ref), custom_call_target="tpu_custom_call" | custom-call | tf_op jit(solution)/shard_map/put_out/pallas_call | solution.py:429

commit v8 on v7

--- a/solution.py
+++ b/solution.py
@@ -116,27 +116,23 @@
 
     def slots(lab_ref, wed_ref, base):
         labels = [lab_ref[p] for p in range(PDEV)]
-        wedges = [wed_ref[p] for p in range(PDEV)]
 
         def one_class(k, carry):
-            p1, w1, p2, w2 = EMPTY, WEDGES, EMPTY, WEDGES
-            seen = jnp.int32(0)
+            p1, p2 = jnp.int32(EMPTY), jnp.int32(-1)
             for p in range(PDEV):
                 hit = labels[p] == k
-                first = hit & (seen == 0)
-                second = hit & (seen > 0)
-                p1 = jnp.where(first, base * 4 + p, p1)
-                w1 = jnp.where(first, wedges[p], w1)
-                p2 = jnp.where(second, base * 4 + p, p2)
-                w2 = jnp.where(second, wedges[p], w2)
-                seen = seen + hit.astype(jnp.int32)
-            slot_p[k * 4 + base] = p1
-            slot_w[k * 4 + base] = w1
-            slot_p[k * 4 + base + 1] = p2
-            slot_w[k * 4 + base + 1] = w2
+                p1 = jnp.where(hit, jnp.minimum(p1, p), p1)
+                p2 = jnp.where(hit, p, p2)
+            one, two = p1 < PDEV, p2 > p1
+            w1 = wed_ref[jnp.minimum(p1, PDEV - 1)]
+            w2 = wed_ref[jnp.maximum(p2, 0)]
+            slot_p[k * 4 + base] = jnp.where(one, base * 4 + p1, EMPTY)
+            slot_w[k * 4 + base] = jnp.where(one, w1, WEDGES)
+            slot_p[k * 4 + base + 1] = jnp.where(two, base * 4 + p2, EMPTY)
+            slot_w[k * 4 + base + 1] = jnp.where(two, w2, WEDGES)
             return carry
 
-        lax.fori_loop(0, 8, one_class, 0)
+        lax.fori_loop(0, 8, one_class, 0, unroll=True)
 
     lab_local.wait()
     wed_local.wait()

time: 25.6 us -> 25.6 us (level)
  no operation moved by 1% of the time
where the time goes in v8:
time: 25.6 us; the launch traced here: 25.3 us
  Pallas kernels  24.7 us (96%)
  between operations  0.64 us (2%)
    pallas_call x1, Pallas kernels, per_device(): pl.pallas_call(kernel, out_shape=shapes, in_specs=[hbm] * 4, out_specs=(v...  24 us
    pallas_call x1, Pallas kernels, per_device(): pl.pallas_call(put_out, out_shape=shapes, in_specs=[vmem] * 2, out_specs=...  0.65 us

profile of v8, /device:TPU:0, one launch (start us, length us, event | category | flops | bytes accessed | tf_op | source)
XLA Modules:
  0.0 25.3 jit_solution(8146649711101990052)
XLA Ops:
  0.6 24.0 %class_sums.1 = (f32[2,27,2,128]{3,2,1,0:T(2,128)S(1)}, f32[27,2,128]{2,1,0:T(2,128)S(1)}) custom-call(s32[8]{0:T(128)} %bitcast.13, s32[8]{0:T(128)} %wed_hbm.1, bf16[8,1728,128]{2,1,0:T(8,128)(2,1)} %bitcast.12, f32[12,110592]{1,0:T(8,128)} %table_hbm.1), custom_call_target="tpu_custom_call" | custom-call | tf_op jit(solution)/shard_map/class_sums/pallas_call | solution.py:401
  24.6 0.6 %put_out.1 = (f32[2,27,2,128]{3,2,1,0:T(2,128)}, f32[27,2,128]{2,1,0:T(2,128)}) custom-call(f32[2,27,2,128]{3,2,1,0:T(2,128)S(1)} %get-tuple-element.6.avg_ref, f32[27,2,128]{2,1,0:T(2,128)S(1)} %get-tuple-element.7.tot_ref), custom_call_target="tpu_custom_call" | custom-call | tf_op jit(solution)/shard_map/put_out/pallas_call | solution.py:425

commit v9 on v7

--- a/solution.py
+++ b/solution.py
@@ -109,9 +109,10 @@
     wed_copy = pltpu.make_async_remote_copy(
         src_ref=wed_hbm, dst_ref=wed_p, send_sem=sem_ls.at[1], recv_sem=sem_lr.at[1],
         device_id=partner, device_id_type=MESH)
-    lab_copy.start()
-    wed_copy.start()
     for pos in range(PIECES):
+        if pos == 3:
+            lab_copy.start()
+            wed_copy.start()
         partner_copy(pos).start()
 
     def slots(lab_ref, wed_ref, base):

time: 25.6 us -> 25.9 us (1.012)
  Pallas kernels: 24.5 us -> 25 us
    pallas_call x1, Pallas kernels: 23.8 us -> 24.4 us  [per_device(): pl.pallas_call(kernel, out_shape=shapes, in_specs=[hbm] * 4, out_specs=(v...]
where the time goes in v9:
time: 25.9 us; the launch traced here: 25.7 us
  Pallas kernels  25 us (97%)
  between operations  0.64 us (2%)
    pallas_call x1, Pallas kernels, per_device(): pl.pallas_call(kernel, out_shape=shapes, in_specs=[hbm] * 4, out_specs=(v...  24.4 us
    pallas_call x1, Pallas kernels, per_device(): pl.pallas_call(put_out, out_shape=shapes, in_specs=[vmem] * 2, out_specs=...  0.65 us

profile of v9, /device:TPU:0, one launch (start us, length us, event | category | flops | bytes accessed | tf_op | source)
XLA Modules:
  0.0 25.7 jit_solution(13419535006749477302)
XLA Ops:
  0.6 24.4 %class_sums.1 = (f32[2,27,2,128]{3,2,1,0:T(2,128)S(1)}, f32[27,2,128]{2,1,0:T(2,128)S(1)}) custom-call(s32[8]{0:T(128)} %bitcast.13, s32[8]{0:T(128)} %wed_hbm.1, bf16[8,1728,128]{2,1,0:T(8,128)(2,1)} %bitcast.12, f32[12,110592]{1,0:T(8,128)} %table_hbm.1), custom_call_target="tpu_custom_call" | custom-call | tf_op jit(solution)/shard_map/class_sums/pallas_call | solution.py:406
  25.0 0.6 %put_out.1 = (f32[2,27,2,128]{3,2,1,0:T(2,128)}, f32[27,2,128]{2,1,0:T(2,128)}) custom-call(f32[2,27,2,128]{3,2,1,0:T(2,128)S(1)} %get-tuple-element.6.avg_ref, f32[27,2,128]{2,1,0:T(2,128)S(1)} %get-tuple-element.7.tot_ref), custom_call_target="tpu_custom_call" | custom-call | tf_op jit(solution)/shard_map/put_out/pallas_call | solution.py:430
